TPU v7x, 32 devices: a whole 2x2x4 slice. The times are simulated.
32 devices in a mesh: dp: 4 (over x, core), expert: 8 (over z, y).
Axes of the slice: x: 2, y: 2, z: 4, core: 2. Of those that a mesh axis runs over, the one named last changes fastest.
Arguments:
- queries: bfloat16 [2, 4, 8, 2048], P(None, 'dp', 'expert'), may hold values from -5 to 5
- cache_keys: bfloat16 [4, 8, 512, 512], P('dp', 'expert'), may hold values from -5 to 5
- cache_values: bfloat16 [4, 8, 512, 512], P('dp', 'expert'), may hold values from -6 to 6
- new_keys: bfloat16 [2, 4, 8, 512], P(None, 'dp', 'expert'), may hold values from -9 to 9
- new_values: bfloat16 [2, 4, 8, 512], P(None, 'dp', 'expert'), may hold values from -6 to 6
- cache_len: int32 [4, 8], P('dp', 'expert'), may hold values from 256 to 510, as said below
- o_proj: bfloat16 [2048, 4096], P(None, 'expert'), may hold values from -0.125 to 0.125
- residual_in: bfloat16 [2, 4, 8, 4096], P(None, 'dp', None, 'expert'), may hold values from -36 to 36
- norm_gain: float32 [4096], P('expert'), may hold values from 0.1 to 1.9
- router: float32 [4096, 8], P('expert'), may hold values from -0.09375 to 0.09375
- expert_gate: bfloat16 [8, 4096, 14336], P('expert', None, 'dp'), may hold values from -0.09375 to 0.09375
- expert_up: bfloat16 [8, 4096, 14336], P('expert', None, 'dp'), may hold values from -0.09375 to 0.09375
- expert_down: bfloat16 [8, 14336, 4096], P('expert', 'dp'), may hold values from -0.046875 to 0.046875
- routes: int32 [2, 4, 8, 2], replicated, may hold values from 0 to 7, all different within a row; in each aligned block of 8 rows (0 to 7, 8 to 15, ..., all dimensions but the last counted through in order) at most 4 rows name the same one
- answers: int32 [2, 4, 8], P(None, 'dp', 'expert'), may hold values from 0 to 127
- stop_mask: int32 [2, 4], P(None, 'dp'), may hold values 0 or 1
Outputs:
- residual_out: bfloat16 [2, 4, 8, 4096], P(None, 'dp', None, 'expert')
- vote_share: float32 [2, 4, 128], P(None, 'dp')
Inputs may be any that keep to these rules, and one draw needn't show every extreme that they name: `cache_len`: some sequence uses exactly 510 cached positions. `routes`: each token names 2 different experts; in each step, the tokens of the 1 prompts of one index of dp (all their samples together) name one expert at most 4 times.
All inputs are finite; a program needn't handle non-finite values. No bound on the sum of `stop_mask` on one device may be relied on, other than what follows from the above.
Results may differ from a plain program's by a relative error of at most 0.0055.
Values may be sent and summed in bfloat16 or wider, within the bound.
No kernel may reach another device: no remote copies, remote signals or barrier semaphores. Data moves between devices by JAX's collectives and lax.ppermute only.
A program may use at most 192 MiB of HBM per device.

v0:
```python
import jax
import jax.numpy as jnp
from jax import lax
from jax.sharding import PartitionSpec as P

D = 4096
E = 8
TOP = 2
HD = 128
QH = 16
KVH = 4
STEPS = 2
ANSWERS = 128


EPSILON = 1e-05


def attend(query, keys, values, fresh_keys, fresh_values, lengths):
    step_count = query.shape[0]
    row_count = query.shape[1]
    cache_size = keys.shape[1]
    group_size = QH // KVH
    score_scale = HD ** (-0.5)
    queried = query.reshape(step_count, row_count, KVH, group_size, HD)
    old_keys = keys.reshape(row_count, cache_size, KVH, HD)
    old_values = values.reshape(row_count, cache_size, KVH, HD)
    young_keys = fresh_keys.reshape(step_count, row_count, KVH, HD)
    young_values = fresh_values.reshape(step_count, row_count, KVH, HD)
    old_scores = (
        jnp.einsum("trkgd,rckd->rkgtc", queried, old_keys, preferred_element_type=jnp.float32)
        * score_scale
    )
    new_scores = (
        jnp.einsum("trkgd,urkd->rkgtu", queried, young_keys, preferred_element_type=jnp.float32)
        * score_scale
    )
    old_valid = jnp.arange(cache_size, dtype=jnp.int32)[None, :] < lengths[:, None]
    old_scores = jnp.where(old_valid[:, None, None, None, :], old_scores, -jnp.inf)
    new_valid = jnp.arange(step_count)[None, :] <= jnp.arange(step_count)[:, None]
    new_scores = jnp.where(new_valid, new_scores, -jnp.inf)
    highest = jnp.maximum(jnp.max(old_scores, -1), jnp.max(new_scores, -1))[..., None]
    old_exp = jnp.exp(old_scores - highest)
    new_exp = jnp.exp(new_scores - highest)
    denominator = jnp.sum(old_exp, -1, keepdims=True) + jnp.sum(new_exp, -1, keepdims=True)
    old_weights = (old_exp / denominator).astype(jnp.bfloat16)
    new_weights = (new_exp / denominator).astype(jnp.bfloat16)
    combined = jnp.einsum(
        "rkgtc,rckd->trkgd", old_weights, old_values, preferred_element_type=jnp.float32
    )
    combined = combined + jnp.einsum(
        "rkgtu,urkd->trkgd", new_weights, young_values, preferred_element_type=jnp.float32
    )
    return combined.reshape(step_count, row_count, QH * HD).astype(jnp.bfloat16)


def slot_tables(picks, capacity):
    block_count = picks.shape[0]
    row_count = picks.shape[1]
    expert_hot = (picks[..., None] == jnp.arange(E, dtype=jnp.int32)).astype(jnp.int32)
    expert_hot = expert_hot.reshape(block_count, row_count * TOP, E)
    earlier = jnp.cumsum(expert_hot, 1) - expert_hot
    place = jnp.sum(earlier * expert_hot, -1).reshape(block_count, row_count, TOP)
    slot_ids = picks * capacity + place
    return (slot_ids[..., None] == jnp.arange(E * capacity, dtype=jnp.int32)).astype(jnp.float32)


def on_device(
    queries,
    cache_keys,
    cache_values,
    new_keys,
    new_values,
    cache_len,
    o_proj,
    residual_in,
    norm_gain,
    router,
    expert_gate,
    expert_up,
    expert_down,
    routes,
    answers,
    stop_mask,
):
    prompt_dev = residual_in.shape[1]
    samples = residual_in.shape[2]
    columns = residual_in.shape[3]
    local_count = queries.shape[2]
    seq_count = prompt_dev * local_count
    cache_size = cache_keys.shape[2]
    spread = lax.axis_size("expert") // E
    capacity = 2 * prompt_dev * samples * TOP // E
    block_rows = prompt_dev * samples
    dp_index = lax.axis_index("dp")
    attended = attend(
        queries.reshape(STEPS, seq_count, QH * HD),
        cache_keys.reshape(seq_count, cache_size, KVH * HD),
        cache_values.reshape(seq_count, cache_size, KVH * HD),
        new_keys.reshape(STEPS, seq_count, KVH * HD),
        new_values.reshape(STEPS, seq_count, KVH * HD),
        cache_len.reshape(seq_count),
    ).reshape(STEPS, prompt_dev, local_count, QH * HD)
    active = (1 - stop_mask).astype(jnp.float32)
    attn_proj = jnp.einsum(
        "tpsq,qc->tpsc",
        lax.all_gather(attended, "expert", axis=2, tiled=True),
        o_proj,
        preferred_element_type=jnp.float32,
    )
    mixed_rows = residual_in.astype(jnp.float32) + attn_proj
    squares = jnp.sum(mixed_rows * mixed_rows, -1)
    scaled = mixed_rows * norm_gain
    squares_all = lax.psum(squares, "expert")
    inv_rms = lax.rsqrt(squares_all / D + EPSILON)[..., None]
    normed_f = scaled * inv_rms
    partial_logits = jnp.einsum("tpsc,ce->tpse", normed_f, router, precision=lax.Precision.HIGHEST)
    logits = lax.psum(partial_logits, "expert")
    normed = normed_f.astype(jnp.bfloat16)
    own_picks = lax.dynamic_slice_in_dim(routes, dp_index * prompt_dev, prompt_dev, 1)
    expert_hot = (own_picks[..., None] == jnp.arange(E, dtype=jnp.int32)).astype(jnp.float32)
    chosen = jnp.sum(expert_hot * logits[:, :, :, None, :], -1)
    gate_weights = jax.nn.sigmoid(chosen - chosen[..., ::-1]).reshape(STEPS, block_rows, TOP)
    own_table = slot_tables(own_picks.reshape(STEPS, block_rows, TOP), capacity)
    senders = jnp.sum(own_table, 2).astype(jnp.bfloat16)
    outgoing = jnp.einsum(
        "trs,trx->tsx",
        senders,
        normed.reshape(STEPS, block_rows, columns),
        preferred_element_type=jnp.float32,
    ).astype(jnp.bfloat16)
    outgoing = jnp.transpose(outgoing.reshape(STEPS, E, capacity, columns), (1, 0, 2, 3)).reshape(
        E, 1, STEPS * capacity, columns
    )
    outgoing = jnp.broadcast_to(outgoing, (E, spread, STEPS * capacity, columns)).reshape(
        E * spread, STEPS * capacity, columns
    )
    tokens = lax.all_gather(
        lax.all_to_all(outgoing, "expert", split_axis=0, concat_axis=2, tiled=True),
        "dp",
        axis=0,
        tiled=True,
    )
    gate_part = jnp.einsum(
        "...d,df->...f", tokens, expert_gate[0], preferred_element_type=jnp.float32
    )
    up_part = jnp.einsum("...d,df->...f", tokens, expert_up[0], preferred_element_type=jnp.float32)
    hidden = (jax.nn.silu(gate_part) * up_part).astype(jnp.bfloat16)
    partial_out = lax.psum_scatter(
        jnp.einsum("...f,fd->...d", hidden, expert_down[0], preferred_element_type=jnp.float32),
        "dp",
        scatter_dimension=0,
        tiled=True,
    )
    returned = lax.all_to_all(partial_out, "expert", split_axis=2, concat_axis=0, tiled=True)
    slot_out = jnp.sum(returned.reshape(E, spread, STEPS, capacity, columns), 1)
    slot_out = jnp.transpose(slot_out, (1, 0, 2, 3)).reshape(STEPS, E * capacity, columns)
    combine = jnp.einsum("trk,trks->trs", gate_weights, own_table)
    moe = jnp.einsum("trs,tsx->trx", combine, slot_out, precision=lax.Precision.HIGHEST).reshape(
        STEPS, prompt_dev, samples, columns
    )
    updated = residual_in.astype(jnp.float32) + active[:, :, None, None] * (attn_proj + moe)
    hits = jnp.sum(
        (answers[..., None] == jnp.arange(ANSWERS, dtype=jnp.int32)).astype(jnp.float32), 2
    )
    votes = active[:, :, None] * hits
    tallied = lax.psum(votes, "expert")
    running = jnp.cumsum(tallied, 0)
    shares = running / jnp.maximum(jnp.sum(running, -1, keepdims=True), 1.0)
    return (updated.astype(jnp.bfloat16), shares)


def solution(mesh):
    placed = (
        P(None, "dp", "expert", None),
        P("dp", "expert", None, None),
        P("dp", "expert", None, None),
        P(None, "dp", "expert", None),
        P(None, "dp", "expert", None),
        P("dp", "expert"),
        P(None, "expert"),
        P(None, "dp", None, "expert"),
        P("expert"),
        P("expert", None),
        P("expert", None, "dp"),
        P("expert", None, "dp"),
        P("expert", "dp", None),
        P(),
        P(None, "dp", "expert"),
        P(None, "dp"),
    )
    return jax.shard_map(
        on_device,
        mesh=mesh,
        in_specs=placed,
        out_specs=(P(None, "dp", None, "expert"), P(None, "dp", None)),
        check_vma=False,
    )
```

profile of v0, /device:TPU:0, one launch (start us, length us, event | category | flops | bytes accessed | tf_op | source)
XLA Modules:
  0.0 199.6 jit_solution(14043567168421434307)
XLA Ops:
  7.2 0.9 reshape.296
  8.1 1.2 reshape.295
  9.9 0.9 convolution_multiply_fusion.1
  10.7 0.1 fusion.62
  10.8 0.3 fusion.63
  11.2 0.1 fusion.55
  11.3 0.2 fusion.37
  11.5 0.1 fusion.58
  11.6 1.2 reshape.299
  12.7 0.3 fusion.26
  13.0 0.9 fusion.25
  13.9 32.4 %all_gather.6 = bf16[2,1,8,2048]{3,0,1,2:T(2,128)(2,1)S(1)} all-gather(bf16[2,1,1,2048]{3,0,1,2:T(2,128)(2,1)S(1)} %bitcast.171), channel_id=1, replica_groups=mesh['dp'=4,'expert'=8] {'expert'}, dimensions={2}, use_global_device_ids=true | all-gather | bytes 73728 | tf_op jit(solution)/shard_map/all_gather | solution.py:107
  46.3 1.2 multiply_reduce_fusion
  47.4 21.3 %psum.21 = f32[2,1,8]{2,0,1:T(2,128)S(1)} all-reduce(f32[2,1,8]{2,0,1:T(2,128)S(1)} %bitcast.173), channel_id=1, replica_groups=mesh['dp'=4,'expert'=8] {'expert'}, use_global_device_ids=true, to_apply=%region_5.6 | all-reduce | flops 16 | bytes 128 | tf_op jit(solution)/shard_map/psum | solution.py:114
  68.8 0.7 constant_dynamic-slice_fusion
  69.5 0.1 copy.110
  69.6 0.1 eq.81
  69.8 0.2 select_reduce_fusion
  70.0 0.1 copy.111
  70.1 0.7 multiply_add_fusion
  70.9 0.9 convolution_convert_fusion
  71.9 0.6 copy.113
  72.5 3.3 %all-to-all-start = ((bf16[8,8,512]{2,1,0:T(8,128)(2,1)}), bf16[8,8,512]{2,1,0:T(8,128)(2,1)S(1)}, u32[]{:S(2)}, u32[]{:S(2)}) async-start(bf16[8,8,512]{2,1,0:T(8,128)(2,1)} %copy.113), calls=%async_computation | async-start | bytes 131072 | tf_op jit(solution)/shard_map/all_to_all | solution.py:139
  75.9 1.0 fusion.38
  76.9 0.7 convert_bitcast_fusion
  77.6 0.7 compare_select_fusion
  78.3 4.4 %all-to-all-done = bf16[8,8,512]{2,1,0:T(8,128)(2,1)S(1)} async-done(((bf16[8,8,512]{2,1,0:T(8,128)(2,1)}), bf16[8,8,512]{2,1,0:T(8,128)(2,1)S(1)}, u32[]{:S(2)}, u32[]{:S(2)}) %all-to-all-start) | async-done | bytes 65568 | tf_op jit(solution)/shard_map/all_to_all | solution.py:139
  82.7 5.8 %all_gather.7 = bf16[4,8,4096]{2,1,0:T(8,128)(2,1)S(1)} all-gather(bf16[1,8,4096]{2,1,0:T(8,128)(2,1)S(1)} %bitcast.169), channel_id=1, replica_groups=mesh['dp'=4,'expert'=8] {'dp'}, dimensions={0}, use_global_device_ids=true | all-gather | bytes 327680 | tf_op jit(solution)/shard_map/all_gather | solution.py:138
  88.5 11.8 %fusion.4 = f32[4,8,3584]{2,1,0:T(8,128)S(1)} fusion(bf16[4,8,4096]{2,1,0:T(8,128)(2,1)S(1)} %all_gather.7, bf16[1,4096,3584]{2,1,0:T(8,128)(2,1)} %param.26), kind=kOutput, calls=%fused_computation.4 | convolution fusion | flops 939524096 | bytes 30081024 | tf_op jit(solution)/shard_map/...d,df->...f/dot_general | solution.py:144
  100.3 22.4 %fusion = f32[4,8,4096]{2,1,0:T(8,128)} fusion(bf16[1,3584,4096]{2,1,0:T(8,128)(2,1)} %param.28, bf16[4,8,4096]{2,1,0:T(8,128)(2,1)S(1)} %all_gather.7, bf16[1,4096,3584]{2,1,0:T(8,128)(2,1)} %param.27, f32[4,8,3584]{2,1,0:T(8,128)S(1)} %fusion.4), kind=kOutput, calls=%fused_computation | convolution fusion | flops 1879736320 | bytes 59965440 | tf_op jit(solution)/shard_map/...f,fd->...d/dot_general | solution.py:150
  122.7 0.7 fusion.72
  123.4 18.6 %all-reduce = (f32[2,8,8]{2,1,0:T(8,128)S(1)}, f32[2,1,128]{2,1,0:T(1,128)S(1)}) all-reduce(f32[2,8,8]{2,1,0:T(8,128)S(1)} %fusion.38, f32[2,1,128]{2,1,0:T(1,128)S(1)} %compare_select_fusion), channel_id=1, replica_groups=mesh['dp'=4,'expert'=8] {'expert'}, use_global_device_ids=true, to_apply=%region_6.7 | all-reduce | flops 384 | bytes 3072 | tf_op jit(solution)/shard_map/psum | solution.py:118
  142.0 0.2 select_reduce_fusion.1
  142.2 0.1 reduce_sum.83
  142.4 4.8 %copy.114 = f32[1,8,4096]{1,0,2:T(1,128)} copy(f32[1,8,4096]{2,1,0:T(8,128)} %reduce-scatter.2.cloned.1.call-done) | data formatting | bytes 262144 | tf_op jit(solution)/shard_map/reduce_scatter | solution.py:149
  147.2 0.5 broadcast.178
  147.7 20.4 %reduce.7 = f32[4096,8]{1,0:T(8,128)} reduce(f32[4096,1,8]{2,1,0:T(1,128)} %bitcast.164, f32[]{:T(128)} %broadcast.178), dimensions={1}, to_apply=%bitcast.149.reduce_sub_computation | reduce | bytes 262148
  168.0 3.3 %reshape.320 = f32[8,1,4096]{2,1,0:T(1,128)} reshape(f32[4096,8]{1,0:T(8,128)} %reduce.7) | data formatting | bytes 262144
  171.3 5.1 %all-to-all-start.1 = ((f32[8,1,4096]{2,1,0:T(1,128)}), f32[8,1,4096]{2,1,0:T(1,128)S(1)}, u32[]{:S(2)}, u32[]{:S(2)}) async-start(f32[8,1,4096]{2,1,0:T(1,128)} %reshape.320), calls=%async_computation.2 | async-start | bytes 262144 | tf_op jit(solution)/shard_map/all_to_all | solution.py:155
  176.5 0.6 broadcast_divide_fusion
  177.1 0.1 copy.122
  177.2 0.1 fusion.42
  177.4 6.5 %all-to-all-done.1 = f32[8,1,4096]{2,1,0:T(1,128)S(1)} async-done(((f32[8,1,4096]{2,1,0:T(1,128)}), f32[8,1,4096]{2,1,0:T(1,128)S(1)}, u32[]{:S(2)}, u32[]{:S(2)}) %all-to-all-start.1) | async-done | bytes 131104 | tf_op jit(solution)/shard_map/all_to_all | solution.py:155
  183.8 1.0 reduce.8
  184.8 4.9 %reshape.321 = f32[4096,1,8]{2,1,0:T(1,128)} reshape(f32[8,4096]{1,0:T(8,128)S(1)} %reduce.8) | data formatting | bytes 262144
  189.6 2.2 %copy.131 = f32[1,8,8,512]{3,2,1,0:T(8,128)S(1)} copy(f32[1,8,8,512]{1,3,2,0:T(8,128)} %bitcast.165) | data formatting | bytes 262144 | tf_op jit(solution)/shard_map/all_to_all | solution.py:155
  191.8 0.1 copy.116
  192.0 0.8 fusion.23
  (26 shorter events, 0.6 us)
Async XLA Ops:
  7.2 39.1 %copy-start = (bf16[2048,512]{1,0:T(8,128)(2,1)S(1)}, bf16[2048,512]{1,0:T(8,128)(2,1)}, u32[]{:S(2)}) copy-start(bf16[2048,512]{1,0:T(8,128)(2,1)} %param.22) | copy-start | bytes 6291460
  72.5 10.2 %all-to-all-start = ((bf16[8,8,512]{2,1,0:T(8,128)(2,1)}), bf16[8,8,512]{2,1,0:T(8,128)(2,1)S(1)}, u32[]{:S(2)}, u32[]{:S(2)}) async-start(bf16[8,8,512]{2,1,0:T(8,128)(2,1)} %copy.113), calls=%async_computation | async-start | bytes 131072 | tf_op jit(solution)/shard_map/all_to_all | solution.py:139
  75.9 66.5 %reduce-scatter.2.cloned.1.call-start = ((), (), s32[]{:S(2)}) async-start(), calls=%async_computation.3 | async-start | bytes 655360 | tf_op jit(solution)/shard_map/reduce_scatter | solution.py:149
  100.3 91.7 %copy-start.1 = (bf16[2,1,8,512]{3,2,1,0:T(8,128)(2,1)S(1)}, bf16[2,1,8,512]{3,2,1,0:T(8,128)(2,1)}, u32[]{:S(2)}) copy-start(bf16[2,1,8,512]{3,2,1,0:T(8,128)(2,1)} %param.23) | copy-start | bytes 49156
  171.3 12.5 %all-to-all-start.1 = ((f32[8,1,4096]{2,1,0:T(1,128)}), f32[8,1,4096]{2,1,0:T(1,128)S(1)}, u32[]{:S(2)}, u32[]{:S(2)}) async-start(f32[8,1,4096]{2,1,0:T(1,128)} %reshape.320), calls=%async_computation.2 | async-start | bytes 262144 | tf_op jit(solution)/shard_map/all_to_all | solution.py:155
Sparse Core Ops, SparseCore 0:
  122.9 19.1 reduce-scatter.1
where the time goes:
time: 201 us; the launch traced here: 200 us
  blocking collectives  78 us (39%)
  matrix products  40.6 us (20%)
  other arithmetic  25.3 us (13%)
  local copies, waits for them, and re-layouts  21.5 us (11%)
  between operations  14.8 us (7%)
  waiting for transfers between devices  10.9 us (5%)
  starting transfers between devices  8.52 us (4%)
    all_gather x1, blocking collectives, on_device(): lax.all_gather(attended, 'expert', axis=2, tiled=True)  32.4 us
    dot_general x1, matrix products, on_device(): jnp.einsum('...f,fd->...d', hidden, expert_down[0], preferred_element_typ...  22.4 us
    psum x1, blocking collectives, on_device(): squares_all = lax.psum(squares, 'expert')  21.3 us
    unnamed x1, other arithmetic  20.4 us
    psum x1, blocking collectives, on_device(): logits = lax.psum(partial_logits, 'expert')  18.6 us
    dot_general x1, matrix products, on_device(): jnp.einsum('...d,df->...f', tokens, expert_gate[0], preferred_element_typ...  11.8 us
    unnamed x7, local copies, waits for them, and re-layouts  8.7 us
    all_to_all x1, waiting for transfers between devices, on_device(): lax.all_to_all(partial_out, 'expert', split_axis=2, concat_axis=0, tiled=...  6.46 us
  transfers between devices with their start and end apart: 3, of which 2 were waited for; matrix products, arithmetic and copies ran while one was open for 2% of the time, Pallas kernels for 0%

commit v1 on v0

v1 whole, which is shorter than its diff:
```python
import jax
import jax.numpy as jnp
from jax import lax
from jax.experimental import pallas as pl
from jax.experimental.pallas import tpu as pltpu
from jax.sharding import PartitionSpec as P

E = 8
TOP = 2
HD = 128
ANSWERS = 128
EPSILON = 1e-05
LANES = 128
BF = jnp.bfloat16
F32 = jnp.float32

VM = pl.BlockSpec(memory_space=pltpu.VMEM)
SM = pl.BlockSpec(memory_space=pltpu.SMEM)
AN = pl.BlockSpec(memory_space=pl.ANY)


def held(x):
    return pltpu.with_memory_space_constraint(x, pltpu.VMEM)


def parked(x):
    return pltpu.with_memory_space_constraint(x, pltpu.HBM)


def contract(a, b, ca, cb):
    return lax.dot_general(a, b, (((ca,), (cb,)), ((), ())), preferred_element_type=F32)


def mebi(size):
    return size >> 20


def params(flops, mib):
    return dict(
        compiler_params=pltpu.CompilerParams(vmem_limit_bytes=mib << 20),
        cost_estimate=pl.CostEstimate(flops=flops, transcendentals=0, bytes_accessed=1 << 20),
    )


def attention(queries, keys, values, new_keys, new_values, lengths, answers, routes, peers, capacity, samples):
    _, _, steps, width = queries.shape
    table_rows = steps * samples
    slot_count = steps * capacity
    cache, kv_width = keys.shape[2:]
    kv_heads, heads = kv_width // HD, width // HD
    group = heads // kv_heads
    tail = cache - 16

    def body(q_ref, k_hbm, v_hbm, nk_ref, nv_ref, len_ref, ans_ref, routes_ref, out_ref, place_ref, expert_ref, k_s, v_s, q_s, o_s, used, sems):
        ck = pltpu.make_async_copy(k_hbm.at[0, 0], k_s, sems.at[0])
        cv = pltpu.make_async_copy(v_hbm.at[0, 0], v_s, sems.at[1])
        ck.start()
        cv.start()
        for t in range(steps):
            q = q_ref[0, 0, t : t + 1, :].astype(F32)
            for h in range(heads):
                k, g = divmod(h, group)
                q_s[pl.ds((k * group + g) * steps + t, 1), :] = q[:, h * HD : (h + 1) * HD]
        prompt = lax.axis_index("dp")
        slot_lane = lax.broadcasted_iota(jnp.int32, (1, E * slot_count), 1)
        expert_lane = lax.broadcasted_iota(jnp.int32, (1, LANES), 1)
        for i in range(steps * E):
            used[i] = 0
        for t in range(steps):

            def one(s, _):
                for k in range(TOP):
                    e = routes_ref[t, prompt, k, s]
                    place = used[t * E + e]
                    used[t * E + e] = place + 1
                    slot = e * slot_count + t * capacity + place
                    n = k * table_rows + t * samples + s
                    place_ref[pl.ds(n, 1), :] = (slot_lane == slot).astype(F32)
                    expert_ref[pl.ds(n, 1), :] = (expert_lane == e).astype(F32)
                return 0

            lax.fori_loop(0, samples, one, 0)
        length = len_ref[0, 0]
        rows = group * steps
        position = lax.broadcasted_iota(jnp.int32, (rows, cache), 1)
        step = lax.broadcasted_iota(jnp.int32, (rows, cache), 0) % steps
        fresh = position - (cache - steps)
        valid = (position < length) | ((fresh >= 0) & (fresh <= step))
        row = lax.broadcasted_iota(jnp.int32, (16, kv_width), 0)

        def refresh(s_ref, new_ref):
            last = s_ref[tail:, :].astype(F32)
            for u in range(steps):
                last = jnp.where(row == 16 - steps + u, new_ref[0, 0, u : u + 1, :].astype(F32), last)
            s_ref[tail:, :] = last.astype(BF)

        ck.wait()
        refresh(k_s, nk_ref)
        weights = []
        for k in range(kv_heads):
            q = q_s[k * rows : (k + 1) * rows, :].astype(BF)
            scores = contract(q, k_s[:, k * HD : (k + 1) * HD], 1, 1) * (HD**-0.5)
            scores = jnp.where(valid, scores, -jnp.inf)
            e = jnp.exp(scores - jnp.max(scores, -1, keepdims=True))
            weights.append((e / jnp.sum(e, -1, keepdims=True)).astype(BF))
        cv.wait()
        refresh(v_s, nv_ref)
        for k in range(kv_heads):
            o = contract(weights[k], v_s[:, k * HD : (k + 1) * HD], 1, 0)
            for g in range(group):
                h = k * group + g
                o_s[:, h * HD : (h + 1) * HD] = o[g * steps : (g + 1) * steps, :]
        lane = lax.broadcasted_iota(jnp.int32, (1, ANSWERS), 1)
        for t in range(steps):
            o_s[t : t + 1, width:] = (lane == ans_ref[0, 0, t]).astype(F32)
        payload = o_s[...].astype(BF)
        for i in range(peers):
            out_ref[i] = payload

    return pl.pallas_call(
        body,
        in_specs=[VM, AN, AN, VM, VM, SM, SM, SM],
        out_specs=[VM] * 3,
        out_shape=[
            jax.ShapeDtypeStruct((peers, steps, width + ANSWERS), BF),
            jax.ShapeDtypeStruct((TOP * table_rows, E * slot_count), F32),
            jax.ShapeDtypeStruct((TOP * table_rows, LANES), F32),
        ],
        scratch_shapes=[
            pltpu.VMEM((cache, kv_width), BF),
            pltpu.VMEM((cache, kv_width), BF),
            pltpu.VMEM((heads * steps, HD), F32),
            pltpu.VMEM((steps, width + ANSWERS), F32),
            pltpu.SMEM((steps * E,), jnp.int32),
            pltpu.SemaphoreType.DMA((2,)),
        ],
        name="attention",
        **params(1 << 36, 3),
    )(queries, parked(keys), parked(values), new_keys, new_values, lengths, answers, routes)


def projection(recv, o_proj, residual, gain, router, places, experts, stops, groups, spread):
    peers, steps, wide = recv.shape
    width = wide - ANSWERS
    columns = o_proj.shape[1]
    samples = residual.shape[2]
    rows = steps * samples
    slots = places.shape[1]
    slot_count = slots // E
    payload = columns + LANES

    def body(
        recv_ref, o_ref, res_ref, gain_ref, router_ref, place_ref, expert_ref, stop_ref, out_ref, attn_ref, vote_ref
    ):
        x = jnp.concatenate([recv_ref[i] for i in range(peers)], 0)
        to = lax.broadcasted_iota(jnp.int32, (rows, rows), 0)
        at = lax.broadcasted_iota(jnp.int32, (rows, rows), 1)
        order = (at == (to % samples) * steps + to // samples).astype(BF)
        x = contract(order, x, 1, 0)
        tally = jnp.zeros((1, ANSWERS), F32)
        for t in range(steps):
            hits = jnp.sum(x[t * samples : (t + 1) * samples, width:], 0, keepdims=True)
            tally = tally + (1 - stop_ref[0, t]).astype(F32) * hits
            vote_ref[t] = tally / jnp.maximum(jnp.sum(tally, -1, keepdims=True), 1.0)
        attn = contract(x[:, :width].astype(BF), o_ref[...], 1, 0)
        attn_ref[...] = attn
        residual = jnp.concatenate([res_ref[t, 0].astype(F32) for t in range(steps)], 0)
        mixed = residual + attn
        squares = jnp.sum(mixed * mixed, -1, keepdims=True)
        scaled = mixed * gain_ref[...]
        logits = lax.dot_general(
            scaled,
            router_ref[...],
            (((1,), (1,)), ((), ())),
            precision=lax.Precision.HIGHEST,
            preferred_element_type=F32,
        )
        hot = expert_ref[:, :E]
        difference = jnp.sum(logits * (hot[:rows] - hot[rows:]), -1, keepdims=True)
        lane = lax.broadcasted_iota(jnp.int32, (rows, LANES), 1)
        stacked = []
        for sign in (1.0, -1.0):
            stats = jnp.where(lane == 0, squares, jnp.where(lane == 1, sign * difference, 0.0))
            high = stats.astype(BF).astype(F32)
            rest = stats - high
            middle = rest.astype(BF).astype(F32)
            low = rest - middle
            stats = high + pltpu.roll(middle, 2, 1) + pltpu.roll(low, 4, 1)
            stacked.append(jnp.concatenate([scaled.astype(BF), stats.astype(BF)], 1))
        by_slot = contract(place_ref[...].astype(BF), jnp.concatenate(stacked, 0), 0, 0).astype(BF)
        for e in range(E):
            block = by_slot[e * slot_count : (e + 1) * slot_count, :]
            for group in range(groups):
                for copy in range(spread):
                    out_ref[group * E * spread + e * spread + copy] = block

    return pl.pallas_call(
        body,
        in_specs=[VM] * 7 + [SM],
        out_specs=[VM] * 3,
        out_shape=[
            jax.ShapeDtypeStruct((groups * peers, slot_count, payload), BF),
            jax.ShapeDtypeStruct((rows, columns), F32),
            jax.ShapeDtypeStruct((steps, 1, ANSWERS), F32),
        ],
        name="projection",
        **params(1 << 36, 3 + mebi(2 * groups * peers * slot_count * payload * 2)),
    )(recv, held(o_proj), held(residual), held(gain), held(router), places, experts, stops)


def expert(recv, gate, up, down, peers, columns):
    groups = recv.shape[0] // peers
    slot_count = recv.shape[1]
    tokens = groups * slot_count
    width, hidden = gate.shape
    block = 512 if hidden % 512 == 0 else hidden
    piece = 256 if block % 256 == 0 else block
    pieces = block // piece
    slots = 2

    def body(recv_ref, g_ref, u_ref, down_hbm, out_ref, x_s, d_s, acc_s, sems):
        def fetch(n):
            at = pl.ds(pl.multiple_of(n * piece, 64), piece)
            return pltpu.make_async_copy(down_hbm.at[0, at, :], d_s.at[n % slots], sems.at[n % slots])

        for n in range(min(slots, hidden // piece)):
            fetch(n).start()
        inverse, weight = [], []
        for i in range(groups):
            total = recv_ref[i * peers, :, columns:].astype(F32)
            for c in range(1, peers):
                total = total + recv_ref[i * peers + c, :, columns:].astype(F32)
            total = total + pltpu.roll(total, LANES - 2, 1) + pltpu.roll(total, LANES - 4, 1)
            inv = lax.rsqrt(total[:, 0:1] / width + EPSILON)
            inverse.append(inv)
            weight.append(1.0 / (1.0 + jnp.exp(-inv * total[:, 1:2])))
        inverse = jnp.concatenate(inverse, 0)
        weight = jnp.concatenate(weight, 0)
        for c in range(peers):
            x_s[:, c * columns : (c + 1) * columns] = jnp.concatenate(
                [recv_ref[i * peers + c, :, :columns] for i in range(groups)], 0
            )
        acc_s[...] = jnp.zeros_like(acc_s)

        def step(i, _):
            at = pl.ds(pl.multiple_of(i * block, LANES if block % LANES == 0 else 1), block)
            g = contract(x_s[...], g_ref[:, at], 1, 0) * inverse
            u = contract(x_s[...], u_ref[:, at], 1, 0) * inverse
            h = (g / (1.0 + jnp.exp(-g)) * u).astype(BF)
            for k in range(pieces):
                n = i * pieces + k
                fetch(n).wait()
                acc_s[...] += contract(h[:, k * piece : (k + 1) * piece], d_s[n % slots], 1, 0)

                @pl.when(n + slots < hidden // piece)
                def _():
                    fetch(n + slots).start()

            return 0

        lax.fori_loop(0, hidden // block, step, 0)
        for c in range(peers):
            mine = (acc_s[:, c * columns : (c + 1) * columns] * weight).astype(BF)
            for i in range(groups):
                out_ref[i * peers + c] = mine[i * slot_count : (i + 1) * slot_count, :]

    return pl.pallas_call(
        body,
        in_specs=[VM, VM, VM, AN],
        out_specs=VM,
        out_shape=jax.ShapeDtypeStruct((groups * peers, slot_count, columns), BF),
        scratch_shapes=[
            pltpu.VMEM((tokens, width), BF),
            pltpu.VMEM((slots, piece, width), BF),
            pltpu.VMEM((tokens, width), F32),
            pltpu.SemaphoreType.DMA((slots,)),
        ],
        name="expert",
        **params(1 << 33, 4 + 2 * mebi(recv.size * 2 + tokens * width * 6)),
    )(recv, held(gate), held(up), parked(down))


def combine(recv, places, attn, residual, stops, groups, spread):
    steps, _, samples, columns = residual.shape
    rows = steps * samples
    peers = E * spread

    def body(recv_ref, place_ref, attn_ref, res_ref, stop_ref, out_ref):
        pick = place_ref[:rows, :]
        for k in range(1, TOP):
            pick = pick + place_ref[k * rows : (k + 1) * rows, :]
        pick = pick.astype(BF)
        moe = jnp.zeros((rows, columns), F32)
        for group in range(groups):
            for copy in range(spread):
                mine = jnp.concatenate([recv_ref[group * peers + e * spread + copy] for e in range(E)], 0)
                moe = moe + contract_rows(pick, mine)
        update = attn_ref[...] + moe
        for t in range(steps):
            active = (1 - stop_ref[0, t]).astype(F32)
            fresh = res_ref[t, 0].astype(F32) + active * update[t * samples : (t + 1) * samples, :]
            out_ref[t, 0] = fresh.astype(BF)

    def contract_rows(pick, mine):
        return contract(pick, mine, 1, 0)

    return pl.pallas_call(
        body,
        in_specs=[VM] * 4 + [SM],
        out_specs=VM,
        out_shape=jax.ShapeDtypeStruct(residual.shape, BF),
        name="combine",
        **params(1 << 26, 3 + mebi(2 * recv.size * 2)),
    )(recv, places, attn, held(residual), stops)


def on_device(
    queries,
    cache_keys,
    cache_values,
    new_keys,
    new_values,
    cache_len,
    o_proj,
    residual_in,
    norm_gain,
    router,
    expert_gate,
    expert_up,
    expert_down,
    routes,
    answers,
    stop_mask,
):
    peers = lax.axis_size("expert")
    groups = lax.axis_size("dp")
    spread = peers // E
    samples, columns = residual_in.shape[2:]
    capacity = 2 * residual_in.shape[1] * samples * TOP // E
    gate, up = expert_gate.reshape(expert_gate.shape[1:]), expert_up.reshape(expert_up.shape[1:])
    stops = stop_mask.T
    payload, places, experts = attention(
        jnp.transpose(queries, (1, 2, 0, 3)),
        cache_keys,
        cache_values,
        jnp.transpose(new_keys, (1, 2, 0, 3)),
        jnp.transpose(new_values, (1, 2, 0, 3)),
        cache_len,
        jnp.transpose(answers, (1, 2, 0)),
        jnp.transpose(routes, (0, 1, 3, 2)),
        peers,
        capacity,
        samples,
    )
    recv = lax.all_to_all(payload, "expert", split_axis=0, concat_axis=0, tiled=True)
    outgoing, attn, votes = projection(
        recv, o_proj, residual_in, norm_gain.reshape(1, columns), router.T, places, experts, stops, groups, spread
    )
    tokens = lax.all_to_all(outgoing, ("dp", "expert"), split_axis=0, concat_axis=0, tiled=True)
    partial = expert(tokens, gate, up, expert_down, peers, columns)
    returned = lax.all_to_all(partial, ("dp", "expert"), split_axis=0, concat_axis=0, tiled=True)
    updated = combine(returned, places, attn, residual_in, stops, groups, spread)
    return updated, votes


def solution(mesh):
    placed = (
        P(None, "dp", "expert", None),
        P("dp", "expert", None, None),
        P("dp", "expert", None, None),
        P(None, "dp", "expert", None),
        P(None, "dp", "expert", None),
        P("dp", "expert"),
        P(None, "expert"),
        P(None, "dp", None, "expert"),
        P("expert"),
        P("expert", None),
        P("expert", None, "dp"),
        P("expert", None, "dp"),
        P("expert", "dp", None),
        P(),
        P(None, "dp", "expert"),
        P(None, "dp"),
    )
    return jax.shard_map(
        on_device,
        mesh=mesh,
        in_specs=placed,
        out_specs=(P(None, "dp", None, "expert"), P(None, "dp", None)),
        check_vma=False,
    )
```

time: 201 us -> 73.9 us (0.37)
  matrix products: 40.6 us -> 0 us
  blocking collectives: 78 us -> 42 us
  other arithmetic: 25.3 us -> 0.01 us
  Pallas kernels: 0 us -> 24.8 us
  local copies, waits for them, and re-layouts: 21.5 us -> 5.07 us
  between operations: 14.8 us -> 1.53 us
  waiting for transfers between devices: 10.9 us -> 0 us
  starting transfers between devices: 8.52 us -> 0 us
    all_to_all x0 -> x3, blocking collectives: none -> 42 us  [the longest x1 14.7 us: on_device(): lax.all_to_all(outgoing, ('dp', 'expert'), split_axis=0, concat_axis=0, t...]
    dot_general x11 -> x0, matrix products: 40.6 us -> none  [the longest x1 22.4 us: on_device(): jnp.einsum('...f,fd->...d', hidden, expert_down[0], preferred_element_typ...]
    psum x2 -> x0, blocking collectives: 39.9 us -> none  [the longest x1 21.3 us: on_device(): squares_all = lax.psum(squares, 'expert')]
    all_gather x2 -> x0, blocking collectives: 38.1 us -> none  [the longest x1 32.4 us: on_device(): lax.all_gather(attended, 'expert', axis=2, tiled=True)]
    pallas_call x0 -> x4, Pallas kernels: none -> 24.8 us  [the longest x1 18.7 us: expert(): pl.pallas_call(body, in_specs=[VM, VM, VM, AN], out_specs=VM, out_shape=j...]
    unnamed x1 -> x2, other arithmetic: 20.4 us -> 0.01 us
    all_to_all x2 -> x0, waiting for transfers between devices: 10.9 us -> none  [the longest x1 6.46 us: on_device(): lax.all_to_all(partial_out, 'expert', split_axis=2, concat_axis=0, tiled=...]
    all_to_all x2 -> x0, starting transfers between devices: 8.48 us -> none  [the longest x1 5.13 us: on_device(): lax.all_to_all(partial_out, 'expert', split_axis=2, concat_axis=0, tiled=...]
  transfers between devices with their start and end apart: 3 -> 0, of which waited for: 2 -> 0; matrix products, arithmetic and copies ran while one was open for 2% -> 0% of each run, Pallas kernels for 0% -> 0%
where the time goes in v1:
time: 73.9 us; the launch traced here: 73.4 us
  blocking collectives  42 us (57%)
  Pallas kernels  24.8 us (34%)
  local copies, waits for them, and re-layouts  5.07 us (7%)
  between operations  1.53 us (2%)
    pallas_call x1, Pallas kernels, expert(): pl.pallas_call(body, in_specs=[VM, VM, VM, AN], out_specs=VM, out_shape=j...  18.7 us
    all_to_all x1, blocking collectives, on_device(): lax.all_to_all(outgoing, ('dp', 'expert'), split_axis=0, concat_axis=0, t...  14.7 us
    all_to_all x1, blocking collectives, on_device(): lax.all_to_all(payload, 'expert', split_axis=0, concat_axis=0, tiled=True)  14.3 us
    all_to_all x1, blocking collectives, on_device(): lax.all_to_all(partial, ('dp', 'expert'), split_axis=0, concat_axis=0, ti...  13 us
    unnamed x48, local copies, waits for them, and re-layouts  5.07 us
    pallas_call x1, Pallas kernels, attention(): pl.pallas_call(body, in_specs=[VM, AN, AN, VM, VM, SM, SM, SM], out_specs...  2.79 us
    pallas_call x1, Pallas kernels, projection(): pl.pallas_call(body, in_specs=[VM] * 7 + [SM], out_specs=[VM] * 3, out_sh...  2 us

profile of v1, /device:TPU:0, one launch (start us, length us, event | category | flops | bytes accessed | tf_op | source)
XLA Modules:
  0.0 73.4 jit_solution(6553648875658889572)
XLA Ops:
  1.3 0.0 copy-start.4
  1.3 0.7 copy-done.4
  2.0 0.7 copy-done.5
  2.7 0.0 copy-start.6
  2.7 0.7 copy-done.6
  3.4 0.0 copy-start.7
  3.4 0.7 copy-done.7
  4.0 0.0 copy-start.9
  4.0 0.7 copy-done.9
  4.7 0.0 copy-start
  4.7 0.0 copy-start.1
  4.7 0.0 slice-start
  4.7 0.0 slice-start.1
  4.7 0.0 slice-start.2
  4.7 0.0 slice-start.3
  4.8 0.0 slice-start.7
  4.8 0.0 slice-start.8
  4.8 0.0 slice-start.9
  4.8 0.0 slice-start.10
  4.8 2.8 %attention.1 = (bf16[8,2,2176]{2,1,0:T(2,128)(2,1)S(1)}, f32[32,64]{1,0:T(8,128)S(1)}, f32[32,128]{1,0:T(8,128)S(1)}) custom-call(bf16[1,1,2,2048]{3,2,1,0:T(2,128)(2,1)S(1)} %bitcast.19, bf16[1,1,512,512]{3,2,1,0:T(8,128)(2,1)} %k_hbm.1, bf16[1,1,512,512]{3,2,1,0:T(8,128)(2,1)} %v_hbm.1, bf16[1,1,2,512]{3,2,1,0:T(2,128)(2,1)S(1)} %bitcast.21, ...), custom_call_target="tpu_custom_call" | custom-call | flops 68719476736 | bytes 1048576 | tf_op jit(solution)/shard_map/attention/pallas_call | solution.py:120
  7.6 14.3 %all_to_all.15.recv_ref = bf16[8,2,2176]{2,1,0:T(2,128)(2,1)S(1)} all-to-all(bf16[8,2,2176]{2,1,0:T(2,128)(2,1)S(1)} %get-tuple-element.8), channel_id=1, replica_groups=mesh['dp'=4,'expert'=8] {'expert'}, dimensions={0} | all-to-all | bytes 139264 | tf_op jit(solution)/shard_map/all_to_all | solution.py:355
  21.9 0.0 copy-done
  21.9 0.0 copy-done.1
  21.9 0.0 copy-done.3
  21.9 0.0 copy-done.8
  21.9 0.0 copy-start.2
  21.9 1.6 %copy-done.2 = bf16[2048,512]{1,0:T(8,128)(2,1)S(1)} copy-done((bf16[2048,512]{1,0:T(8,128)(2,1)S(1)}, bf16[2048,512]{1,0:T(8,128)(2,1)}, u32[]{:S(2)}) %copy-start.2) | copy-done | bytes 2097176
  23.5 0.0 slice-start.12
  23.5 0.0 slice-start.13
  23.5 2.0 %projection.1 = (bf16[32,8,640]{2,1,0:T(8,128)(2,1)S(1)}, f32[16,512]{1,0:T(8,128)S(1)}, f32[2,1,128]{2,1,0:T(1,128)}) custom-call(bf16[8,2,2176]{2,1,0:T(2,128)(2,1)S(1)} %all_to_all.15.recv_ref, bf16[2048,512]{1,0:T(8,128)(2,1)S(1)} %copy-done.2, bf16[2,1,8,512]{3,2,1,0:T(8,128)(2,1)S(1)} %copy-done, f32[1,512]{1,0:T(1,128)S(1)} %bitcast.23, ...), custom_call_target="tpu_custom_call" | custom-call | flops 68719476736 | bytes 1048576 | tf_op jit(solution)/shard_map/projection/pallas_call | solution.py:197
  25.5 14.7 %all_to_all.16.recv_ref = bf16[32,8,640]{2,1,0:T(8,128)(2,1)} all-to-all(bf16[32,8,640]{2,1,0:T(8,128)(2,1)S(1)} %get-tuple-element.11), channel_id=1, replica_groups=mesh['dp'=4,'expert'=8] {'dp','expert'}, dimensions={0} | all-to-all | bytes 655360 | tf_op jit(solution)/shard_map/all_to_all | solution.py:359
  40.2 0.0 slice-done
  40.2 0.0 slice-done.1
  40.2 0.0 slice-done.2
  40.2 0.0 slice-done.3
  40.2 0.0 slice-done.7
  40.2 0.0 slice-done.8
  40.2 0.0 slice-done.9
  40.3 0.0 slice-done.10
  40.3 0.0 slice-done.4
  40.3 0.0 slice-done.5
  40.3 0.0 slice-done.6
  40.3 0.0 slice-done.11
  40.3 0.0 slice-done.12
  40.3 0.0 slice-done.13
  40.3 18.7 %expert.1 = bf16[32,8,512]{2,1,0:T(8,128)(2,1)} custom-call(bf16[32,8,640]{2,1,0:T(8,128)(2,1)} %all_to_all.16.recv_ref, bf16[4096,3584]{1,0:T(8,128)(2,1)S(1)} %bitcast.12, bf16[4096,3584]{1,0:T(8,128)(2,1)S(1)} %bitcast.15, bf16[1,3584,4096]{2,1,0:T(8,128)(2,1)} %down_hbm.1), custom_call_target="tpu_custom_call" | custom-call | flops 8589934592 | bytes 1048576 | tf_op jit(solution)/shard_map/expert/pallas_call | solution.py:267
  59.1 13.0 %all_to_all.17.recv_ref = bf16[32,8,512]{2,1,0:T(8,128)(2,1)S(1)} all-to-all(bf16[32,8,512]{2,1,0:T(8,128)(2,1)} %expert.1), channel_id=1, replica_groups=mesh['dp'=4,'expert'=8] {'dp','expert'}, dimensions={0} | all-to-all | bytes 524288 | tf_op jit(solution)/shard_map/all_to_all | solution.py:361
  72.1 1.3 %combine.1 = bf16[2,1,8,512]{3,2,1,0:T(8,128)(2,1)} custom-call(bf16[32,8,512]{2,1,0:T(8,128)(2,1)S(1)} %all_to_all.17.recv_ref, f32[32,64]{1,0:T(8,128)S(1)} %get-tuple-element.9.place_ref, f32[16,512]{1,0:T(8,128)S(1)} %get-tuple-element.12.attn_ref, bf16[2,1,8,512]{3,2,1,0:T(8,128)(2,1)S(1)} %copy-done, s32[1,2]{1,0:T(1,128)S(1)} %bitcast.17), custom_call_target="tpu_custom_call" | custom-call | flops 67108864 | bytes 1048576 | tf_op jit(solution)/shard_map/combine/pallas_call | solution.py:307
  (9 shorter events, 0.0 us)
Async XLA Ops:
  1.3 0.7 copy-start.4
  2.0 0.7 copy-start.5
  2.7 0.7 copy-start.6
  3.4 0.7 copy-start.7
  4.0 0.7 copy-start.9
  4.7 17.2 %copy-start = (bf16[2,1,8,512]{3,2,1,0:T(8,128)(2,1)S(1)}, bf16[2,1,8,512]{3,2,1,0:T(8,128)(2,1)}, u32[]{:S(2)}) copy-start(bf16[2,1,8,512]{3,2,1,0:T(8,128)(2,1)} %res_ref.3) | copy-start | bytes 49156
  4.7 17.2 %copy-start.1 = (s32[2,1]{0,1:T(1,128)S(1)}, s32[2,1]{0,1:T(1,128)}, u32[]{:S(2)}) copy-start(s32[2,1]{0,1:T(1,128)} %param.31) | copy-start | bytes 28
  4.7 17.2 %copy-start.3 = (f32[512,8]{0,1:T(8,128)S(1)}, f32[512,8]{0,1:T(8,128)}, u32[]{:S(2)}) copy-start(f32[512,8]{0,1:T(8,128)} %param.25) | copy-start | bytes 49156
  4.7 17.2 %copy-start.8 = (f32[512]{0:T(512)S(1)}, f32[512]{0:T(512)}, u32[]{:S(2)}) copy-start(f32[512]{0:T(512)} %param.24) | copy-start | bytes 6148
  4.7 35.5 %slice-start = ((s8[29360128]{0:T(1024)(128)(4,1)}), s8[4194304]{0:T(1024)(128)(4,1)S(1)}, s32[]{:S(2)}) async-start(s8[29360128]{0:T(1024)(128)(4,1)} %bitcast.10), calls=%async_computation.3 | async-start | bytes 8388608
  4.7 35.5 %slice-start.1 = ((s8[29360128]{0:T(1024)(128)(4,1)}), s8[4194304]{0:T(1024)(128)(4,1)S(1)}, s32[]{:S(2)}) async-start(s8[29360128]{0:T(1024)(128)(4,1)} %bitcast.10), calls=%async_computation.4 | async-start | bytes 8388608
  4.7 35.5 %slice-start.2 = ((s8[29360128]{0:T(1024)(128)(4,1)}), s8[4194304]{0:T(1024)(128)(4,1)S(1)}, s32[]{:S(2)}) async-start(s8[29360128]{0:T(1024)(128)(4,1)} %bitcast.10), calls=%async_computation.5 | async-start | bytes 8388608
  4.7 35.5 %slice-start.3 = ((s8[29360128]{0:T(1024)(128)(4,1)}), s8[4194304]{0:T(1024)(128)(4,1)S(1)}, s32[]{:S(2)}) async-start(s8[29360128]{0:T(1024)(128)(4,1)} %bitcast.10), calls=%async_computation.6 | async-start | bytes 8388608
  4.8 35.5 %slice-start.7 = ((s8[29360128]{0:T(1024)(128)(4,1)}), s8[4194304]{0:T(1024)(128)(4,1)S(1)}, s32[]{:S(2)}) async-start(s8[29360128]{0:T(1024)(128)(4,1)} %bitcast.13), calls=%async_computation.10 | async-start | bytes 8388608
  4.8 35.5 %slice-start.8 = ((s8[29360128]{0:T(1024)(128)(4,1)}), s8[4194304]{0:T(1024)(128)(4,1)S(1)}, s32[]{:S(2)}) async-start(s8[29360128]{0:T(1024)(128)(4,1)} %bitcast.13), calls=%async_computation.11 | async-start | bytes 8388608
  4.8 35.5 %slice-start.9 = ((s8[29360128]{0:T(1024)(128)(4,1)}), s8[4194304]{0:T(1024)(128)(4,1)S(1)}, s32[]{:S(2)}) async-start(s8[29360128]{0:T(1024)(128)(4,1)} %bitcast.13), calls=%async_computation.12 | async-start | bytes 8388608
  4.8 35.5 %slice-start.10 = ((s8[29360128]{0:T(1024)(128)(4,1)}), s8[4194304]{0:T(1024)(128)(4,1)S(1)}, s32[]{:S(2)}) async-start(s8[29360128]{0:T(1024)(128)(4,1)} %bitcast.13), calls=%async_computation.13 | async-start | bytes 8388608
  21.9 1.6 %copy-start.2 = (bf16[2048,512]{1,0:T(8,128)(2,1)S(1)}, bf16[2048,512]{1,0:T(8,128)(2,1)}, u32[]{:S(2)}) copy-start(bf16[2048,512]{1,0:T(8,128)(2,1)} %o_ref.1) | copy-start | bytes 6291460
  23.5 16.7 %slice-start.4 = ((s8[29360128]{0:T(1024)(128)(4,1)}), s8[4194304]{0:T(1024)(128)(4,1)S(1)}, s32[]{:S(2)}) async-start(s8[29360128]{0:T(1024)(128)(4,1)} %bitcast.10), calls=%async_computation.7 | async-start | bytes 8388608
  23.5 16.8 %slice-start.5 = ((s8[29360128]{0:T(1024)(128)(4,1)}), s8[4194304]{0:T(1024)(128)(4,1)S(1)}, s32[]{:S(2)}) async-start(s8[29360128]{0:T(1024)(128)(4,1)} %bitcast.10), calls=%async_computation.8 | async-start | bytes 8388608
  23.5 16.8 %slice-start.6 = ((s8[29360128]{0:T(1024)(128)(4,1)}), s8[4194304]{0:T(1024)(128)(4,1)S(1)}, s32[]{:S(2)}) async-start(s8[29360128]{0:T(1024)(128)(4,1)} %bitcast.10), calls=%async_computation.9 | async-start | bytes 8388608
  23.5 16.8 %slice-start.11 = ((s8[29360128]{0:T(1024)(128)(4,1)}), s8[4194304]{0:T(1024)(128)(4,1)S(1)}, s32[]{:S(2)}) async-start(s8[29360128]{0:T(1024)(128)(4,1)} %bitcast.13), calls=%async_computation.14 | async-start | bytes 8388608
  23.5 16.8 %slice-start.12 = ((s8[29360128]{0:T(1024)(128)(4,1)}), s8[4194304]{0:T(1024)(128)(4,1)S(1)}, s32[]{:S(2)}) async-start(s8[29360128]{0:T(1024)(128)(4,1)} %bitcast.13), calls=%async_computation.15 | async-start | bytes 8388608
  23.5 16.8 %slice-start.13 = ((s8[29360128]{0:T(1024)(128)(4,1)}), s8[4194304]{0:T(1024)(128)(4,1)S(1)}, s32[]{:S(2)}) async-start(s8[29360128]{0:T(1024)(128)(4,1)} %bitcast.13), calls=%async_computation.16 | async-start | bytes 8388608

commit v2 on v1

--- a/solution.py
+++ b/solution.py
@@ -37,30 +37,42 @@
 
 def params(flops, mib):
     return dict(
-        compiler_params=pltpu.CompilerParams(vmem_limit_bytes=mib << 20),
+        compiler_params=pltpu.CompilerParams(vmem_limit_bytes=int(mib * (1 << 20))),
         cost_estimate=pl.CostEstimate(flops=flops, transcendentals=0, bytes_accessed=1 << 20),
     )
 
 
-def attention(queries, keys, values, new_keys, new_values, lengths, answers, routes, peers, capacity, samples):
+def attention(queries, keys, values, new_keys, new_values, lengths, answers, routes, o_proj, peers, capacity, samples):
     _, _, steps, width = queries.shape
     table_rows = steps * samples
     slot_count = steps * capacity
     cache, kv_width = keys.shape[2:]
     kv_heads, heads = kv_width // HD, width // HD
     group = heads // kv_heads
-    tail = cache - 16
-
-    def body(q_ref, k_hbm, v_hbm, nk_ref, nv_ref, len_ref, ans_ref, routes_ref, out_ref, place_ref, expert_ref, k_s, v_s, q_s, o_s, used, sems):
-        ck = pltpu.make_async_copy(k_hbm.at[0, 0], k_s, sems.at[0])
-        cv = pltpu.make_async_copy(v_hbm.at[0, 0], v_s, sems.at[1])
-        ck.start()
-        cv.start()
-        for t in range(steps):
-            q = q_ref[0, 0, t : t + 1, :].astype(F32)
-            for h in range(heads):
-                k, g = divmod(h, group)
-                q_s[pl.ds((k * group + g) * steps + t, 1), :] = q[:, h * HD : (h + 1) * HD]
+    rows = group * steps
+    first = cache - steps
+
+    def body(
+        q_ref,
+        k_ref,
+        v_ref,
+        nk_ref,
+        nv_ref,
+        len_ref,
+        ans_ref,
+        routes_ref,
+        o_hbm,
+        out_ref,
+        place_ref,
+        expert_ref,
+        o_ref,
+        q_s,
+        a_s,
+        used,
+        sem,
+    ):
+        move = pltpu.make_async_copy(o_hbm, o_ref, sem)
+        move.start()
         prompt = lax.axis_index("dp")
         slot_lane = lax.broadcasted_iota(jnp.int32, (1, E * slot_count), 1)
         expert_lane = lax.broadcasted_iota(jnp.int32, (1, LANES), 1)
@@ -80,63 +92,65 @@
                 return 0
 
             lax.fori_loop(0, samples, one, 0)
-        length = len_ref[0, 0]
-        rows = group * steps
+        for t in range(steps):
+            q = q_ref[0, 0, t : t + 1, :].astype(F32)
+            for h in range(heads):
+                q_s[pl.ds(h * steps + t, 1), :] = q[:, h * HD : (h + 1) * HD]
         position = lax.broadcasted_iota(jnp.int32, (rows, cache), 1)
         step = lax.broadcasted_iota(jnp.int32, (rows, cache), 0) % steps
-        fresh = position - (cache - steps)
-        valid = (position < length) | ((fresh >= 0) & (fresh <= step))
-        row = lax.broadcasted_iota(jnp.int32, (16, kv_width), 0)
-
-        def refresh(s_ref, new_ref):
-            last = s_ref[tail:, :].astype(F32)
+        fresh = position - first
+        valid = (position < len_ref[0, 0]) | ((fresh >= 0) & (fresh <= step))
+        new_keys = nk_ref[0, 0].astype(F32)
+        new_values = nv_ref[0, 0].astype(F32)
+        for k in range(kv_heads):
+            at = slice(k * HD, (k + 1) * HD)
+            q = q_s[k * rows : (k + 1) * rows, :]
+            scores = contract(q.astype(BF), k_ref[0, 0, :, at], 1, 1)
             for u in range(steps):
-                last = jnp.where(row == 16 - steps + u, new_ref[0, 0, u : u + 1, :].astype(F32), last)
-            s_ref[tail:, :] = last.astype(BF)
-
-        ck.wait()
-        refresh(k_s, nk_ref)
-        weights = []
-        for k in range(kv_heads):
-            q = q_s[k * rows : (k + 1) * rows, :].astype(BF)
-            scores = contract(q, k_s[:, k * HD : (k + 1) * HD], 1, 1) * (HD**-0.5)
-            scores = jnp.where(valid, scores, -jnp.inf)
+                score = jnp.sum(q * new_keys[u : u + 1, at], -1, keepdims=True)
+                scores = jnp.where(fresh == u, score, scores)
+            scores = jnp.where(valid, scores * (HD**-0.5), -jnp.inf)
             e = jnp.exp(scores - jnp.max(scores, -1, keepdims=True))
-            weights.append((e / jnp.sum(e, -1, keepdims=True)).astype(BF))
-        cv.wait()
-        refresh(v_s, nv_ref)
-        for k in range(kv_heads):
-            o = contract(weights[k], v_s[:, k * HD : (k + 1) * HD], 1, 0)
+            weights = (e / jnp.sum(e, -1, keepdims=True)).astype(BF)
+            o = contract(jnp.where(fresh < 0, weights, jnp.zeros_like(weights)), v_ref[0, 0, :, at], 1, 0)
+            weights = weights.astype(F32)
+            for u in range(steps):
+                weight = jnp.sum(jnp.where(fresh == u, weights, 0.0), -1, keepdims=True)
+                o = o + weight * new_values[u : u + 1, at]
             for g in range(group):
                 h = k * group + g
-                o_s[:, h * HD : (h + 1) * HD] = o[g * steps : (g + 1) * steps, :]
+                a_s[:, h * HD : (h + 1) * HD] = o[g * steps : (g + 1) * steps, :]
         lane = lax.broadcasted_iota(jnp.int32, (1, ANSWERS), 1)
         for t in range(steps):
-            o_s[t : t + 1, width:] = (lane == ans_ref[0, 0, t]).astype(F32)
-        payload = o_s[...].astype(BF)
+            a_s[t : t + 1, width:] = (lane == ans_ref[0, 0, t]).astype(F32)
+        payload = a_s[...].astype(BF)
         for i in range(peers):
             out_ref[i] = payload
+        move.wait()
 
     return pl.pallas_call(
         body,
-        in_specs=[VM, AN, AN, VM, VM, SM, SM, SM],
-        out_specs=[VM] * 3,
+        in_specs=[VM, VM, VM, VM, VM, SM, SM, SM, AN],
+        out_specs=[VM] * 4,
         out_shape=[
             jax.ShapeDtypeStruct((peers, steps, width + ANSWERS), BF),
             jax.ShapeDtypeStruct((TOP * table_rows, E * slot_count), F32),
             jax.ShapeDtypeStruct((TOP * table_rows, LANES), F32),
+            pltpu.VMEM(o_proj.shape, o_proj.dtype),
         ],
         scratch_shapes=[
-            pltpu.VMEM((cache, kv_width), BF),
-            pltpu.VMEM((cache, kv_width), BF),
             pltpu.VMEM((heads * steps, HD), F32),
             pltpu.VMEM((steps, width + ANSWERS), F32),
             pltpu.SMEM((steps * E,), jnp.int32),
-            pltpu.SemaphoreType.DMA((2,)),
+            pltpu.SemaphoreType.DMA,
         ],
         name="attention",
-        **params(1 << 36, 3),
-    )(queries, parked(keys), parked(values), new_keys, new_values, lengths, answers, routes)
+        **params(1 << 36, 2),
+    )(
+        *[parked(x) for x in (queries, keys, values, new_keys, new_values)],
+        lengths,
+        *[parked(x) for x in (answers, routes, o_proj)],
+    )
 
 
 def projection(recv, o_proj, residual, gain, router, places, experts, stops, groups, spread):
@@ -204,7 +218,7 @@
             jax.ShapeDtypeStruct((steps, 1, ANSWERS), F32),
         ],
         name="projection",
-        **params(1 << 36, 3 + mebi(2 * groups * peers * slot_count * payload * 2)),
+        **params(1 << 36, 2 + mebi(2 * groups * peers * slot_count * payload * 2)),
     )(recv, held(o_proj), held(residual), held(gain), held(router), places, experts, stops)
 
 
@@ -214,16 +228,17 @@
     tokens = groups * slot_count
     width, hidden = gate.shape
     block = 512 if hidden % 512 == 0 else hidden
-    piece = 256 if block % 256 == 0 else block
-    pieces = block // piece
-    slots = 2
+    blocks = hidden // block
+    piece = 128 if block % 128 == 0 else block
+    pieces = hidden // piece
+    slots = min(5, pieces)
 
     def body(recv_ref, g_ref, u_ref, down_hbm, out_ref, x_s, d_s, acc_s, sems):
         def fetch(n):
-            at = pl.ds(pl.multiple_of(n * piece, 64), piece)
+            at = pl.ds(n * piece, piece)
             return pltpu.make_async_copy(down_hbm.at[0, at, :], d_s.at[n % slots], sems.at[n % slots])
 
-        for n in range(min(slots, hidden // piece)):
+        for n in range(slots):
             fetch(n).start()
         inverse, weight = [], []
         for i in range(groups):
@@ -240,25 +255,23 @@
             x_s[:, c * columns : (c + 1) * columns] = jnp.concatenate(
                 [recv_ref[i * peers + c, :, :columns] for i in range(groups)], 0
             )
-        acc_s[...] = jnp.zeros_like(acc_s)
-
-        def step(i, _):
-            at = pl.ds(pl.multiple_of(i * block, LANES if block % LANES == 0 else 1), block)
+        def hidden_of(i):
+            at = slice(i * block, (i + 1) * block)
             g = contract(x_s[...], g_ref[:, at], 1, 0) * inverse
             u = contract(x_s[...], u_ref[:, at], 1, 0) * inverse
-            h = (g / (1.0 + jnp.exp(-g)) * u).astype(BF)
-            for k in range(pieces):
-                n = i * pieces + k
+            return (g / (1.0 + jnp.exp(-g)) * u).astype(BF)
+
+        state = hidden_of(0)
+        for i in range(1, blocks + 1):
+            after = hidden_of(i) if i < blocks else None
+            for n in range((i - 1) * block // piece, i * block // piece):
                 fetch(n).wait()
-                acc_s[...] += contract(h[:, k * piece : (k + 1) * piece], d_s[n % slots], 1, 0)
-
-                @pl.when(n + slots < hidden // piece)
-                def _():
+                at = n * piece - (i - 1) * block
+                out = contract(state[:, at : at + piece], d_s[n % slots], 1, 0)
+                acc_s[...] = out if n == 0 else acc_s[...] + out
+                if n + slots < pieces:
                     fetch(n + slots).start()
-
-            return 0
-
-        lax.fori_loop(0, hidden // block, step, 0)
+            state = after
         for c in range(peers):
             mine = (acc_s[:, c * columns : (c + 1) * columns] * weight).astype(BF)
             for i in range(groups):
@@ -268,7 +281,7 @@
         body,
         in_specs=[VM, VM, VM, AN],
         out_specs=VM,
-        out_shape=jax.ShapeDtypeStruct((groups * peers, slot_count, columns), BF),
+        out_shape=pltpu.VMEM((groups * peers, slot_count, columns), BF),
         scratch_shapes=[
             pltpu.VMEM((tokens, width), BF),
             pltpu.VMEM((slots, piece, width), BF),
@@ -276,8 +289,8 @@
             pltpu.SemaphoreType.DMA((slots,)),
         ],
         name="expert",
-        **params(1 << 33, 4 + 2 * mebi(recv.size * 2 + tokens * width * 6)),
-    )(recv, held(gate), held(up), parked(down))
+        **params(1 << 33, 4.5 + 2 * mebi(recv.size * 2 + tokens * width * 6)),
+    )(held(recv), held(gate), held(up), parked(down))
 
 
 def combine(recv, places, attn, residual, stops, groups, spread):
@@ -339,7 +352,7 @@
     capacity = 2 * residual_in.shape[1] * samples * TOP // E
     gate, up = expert_gate.reshape(expert_gate.shape[1:]), expert_up.reshape(expert_up.shape[1:])
     stops = stop_mask.T
-    payload, places, experts = attention(
+    payload, places, experts, o_v = attention(
         jnp.transpose(queries, (1, 2, 0, 3)),
         cache_keys,
         cache_values,
@@ -348,13 +361,14 @@
         cache_len,
         jnp.transpose(answers, (1, 2, 0)),
         jnp.transpose(routes, (0, 1, 3, 2)),
+        o_proj,
         peers,
         capacity,
         samples,
     )
     recv = lax.all_to_all(payload, "expert", split_axis=0, concat_axis=0, tiled=True)
     outgoing, attn, votes = projection(
-        recv, o_proj, residual_in, norm_gain.reshape(1, columns), router.T, places, experts, stops, groups, spread
+        recv, o_v, residual_in, norm_gain.reshape(1, columns), router.T, places, experts, stops, groups, spread
     )
     tokens = lax.all_to_all(outgoing, ("dp", "expert"), split_axis=0, concat_axis=0, tiled=True)
     partial = expert(tokens, gate, up, expert_down, peers, columns)

time: 73.9 us -> 66.5 us (0.90)
  local copies, waits for them, and re-layouts: 5.07 us -> 0.1 us
  blocking collectives: 42 us -> 40.9 us
  Pallas kernels: 24.8 us -> 23.8 us
    unnamed x48 -> x36, local copies, waits for them, and re-layouts: 5.07 us -> 0.1 us
    pallas_call x2, Pallas kernels: 21.5 us -> 20.5 us  [the longest x1 16.8 us: expert(): pl.pallas_call(body, in_specs=[VM, VM, VM, AN], out_specs=VM, out_shape=p...]
where the time goes in v2:
time: 66.5 us; the launch traced here: 66.3 us
  blocking collectives  40.9 us (62%)
  Pallas kernels  23.8 us (36%)
  between operations  1.56 us (2%)
    pallas_call x1, Pallas kernels, expert(): pl.pallas_call(body, in_specs=[VM, VM, VM, AN], out_specs=VM, out_shape=p...  16.8 us
    all_to_all x1, blocking collectives, on_device(): lax.all_to_all(payload, 'expert', split_axis=0, concat_axis=0, tiled=True)  14.3 us
    all_to_all x1, blocking collectives, on_device(): lax.all_to_all(outgoing, ('dp', 'expert'), split_axis=0, concat_axis=0, t...  14 us
    all_to_all x1, blocking collectives, on_device(): lax.all_to_all(partial, ('dp', 'expert'), split_axis=0, concat_axis=0, ti...  12.6 us
    pallas_call x1, Pallas kernels, attention(): pl.pallas_call(body, in_specs=[VM, VM, VM, VM, VM, SM, SM, SM, AN], out_s...  3.68 us
    pallas_call x1, Pallas kernels, projection(): pl.pallas_call(body, in_specs=[VM] * 7 + [SM], out_specs=[VM] * 3, out_sh...  2 us

profile of v2, /device:TPU:0, one launch (start us, length us, event | category | flops | bytes accessed | tf_op | source)
XLA Modules:
  0.0 66.3 jit_solution(16891372009663068680)
XLA Ops:
  1.3 0.0 copy-start
  1.3 0.0 copy-start.1
  1.3 0.0 copy-start.2
  1.3 0.0 copy-start.3
  1.3 0.0 slice-start
  1.3 0.0 slice-start.1
  1.3 0.0 slice-start.2
  1.4 0.0 slice-start.3
  1.4 0.0 slice-start.7
  1.4 0.0 slice-start.8
  1.4 0.0 slice-start.9
  1.4 0.0 slice-start.10
  1.4 3.7 %attention.1 = (bf16[8,2,2176]{2,1,0:T(2,128)(2,1)S(1)}, f32[32,64]{1,0:T(8,128)S(1)}, f32[32,128]{1,0:T(8,128)S(1)}, bf16[2048,512]{1,0:T(8,128)(2,1)S(1)}) custom-call(bf16[1,1,2,2048]{3,2,1,0:T(2,128)(2,1)} %bitcast.20, bf16[1,1,512,512]{3,2,1,0:T(8,128)(2,1)} %k_ref.1, bf16[1,1,512,512]{3,2,1,0:T(8,128)(2,1)} %v_ref.1, bf16[1,1,2,512]{3,2,1,0:T(2,128)(2,1)} %bitcast.22, ...), custom_call_target="tpu_custom_call" | custom-call | flops 68719476736 | bytes 1048576 | tf_op jit(solution)/shard_map/attention/pallas_call | solution.py:131
  5.1 14.3 %all_to_all.15.recv_ref = bf16[8,2,2176]{2,1,0:T(2,128)(2,1)S(1)} all-to-all(bf16[8,2,2176]{2,1,0:T(2,128)(2,1)S(1)} %get-tuple-element.9), channel_id=1, replica_groups=mesh['dp'=4,'expert'=8] {'expert'}, dimensions={0} | all-to-all | bytes 139264 | tf_op jit(solution)/shard_map/all_to_all | solution.py:369
  19.4 0.0 copy-done
  19.4 0.0 copy-done.1
  19.4 0.0 copy-done.2
  19.4 0.0 copy-done.3
  19.4 0.0 slice-start.4
  19.4 0.0 slice-start.5
  19.4 0.0 slice-start.6
  19.5 0.0 slice-start.11
  19.5 0.0 slice-start.12
  19.5 0.0 slice-start.13
  19.5 2.0 %projection.1 = (bf16[32,8,640]{2,1,0:T(8,128)(2,1)S(1)}, f32[16,512]{1,0:T(8,128)S(1)}, f32[2,1,128]{2,1,0:T(1,128)}) custom-call(bf16[8,2,2176]{2,1,0:T(2,128)(2,1)S(1)} %all_to_all.15.recv_ref, bf16[2048,512]{1,0:T(8,128)(2,1)S(1)} %get-tuple-element.10.o_ref, bf16[2,1,8,512]{3,2,1,0:T(8,128)(2,1)S(1)} %copy-done, f32[1,512]{1,0:T(1,128)S(1)} %bitcast.19, ...), custom_call_target="tpu_custom_call" | custom-call | flops 68719476736 | bytes 1048576 | tf_op jit(solution)/shard_map/projection/pallas_call | solution.py:211
  21.5 14.0 %all_to_all.16.recv_ref = bf16[32,8,640]{2,1,0:T(8,128)(2,1)S(1)} all-to-all(bf16[32,8,640]{2,1,0:T(8,128)(2,1)S(1)} %get-tuple-element.13), channel_id=1, replica_groups=mesh['dp'=4,'expert'=8] {'dp','expert'}, dimensions={0} | all-to-all | bytes 655360 | tf_op jit(solution)/shard_map/all_to_all | solution.py:373
  35.5 0.0 slice-done
  35.5 0.0 slice-done.1
  35.5 0.0 slice-done.2
  35.5 0.0 slice-done.3
  35.5 0.0 slice-done.7
  35.5 0.0 slice-done.8
  35.5 0.0 slice-done.9
  35.5 0.0 slice-done.10
  35.5 0.0 slice-done.4
  35.5 0.0 slice-done.5
  35.5 0.0 slice-done.6
  35.6 0.0 slice-done.11
  35.6 0.0 slice-done.12
  35.6 0.0 slice-done.13
  35.6 16.8 %expert.1 = bf16[32,8,512]{2,1,0:T(8,128)(2,1)S(1)} custom-call(bf16[32,8,640]{2,1,0:T(8,128)(2,1)S(1)} %all_to_all.16.recv_ref, bf16[4096,3584]{1,0:T(8,128)(2,1)S(1)} %bitcast.12, bf16[4096,3584]{1,0:T(8,128)(2,1)S(1)} %bitcast.15, bf16[1,3584,4096]{2,1,0:T(8,128)(2,1)} %down_hbm.1), custom_call_target="tpu_custom_call" | custom-call | flops 8589934592 | bytes 1048576 | tf_op jit(solution)/shard_map/expert/pallas_call | solution.py:280
  52.4 12.6 %all_to_all.17.recv_ref = bf16[32,8,512]{2,1,0:T(8,128)(2,1)S(1)} all-to-all(bf16[32,8,512]{2,1,0:T(8,128)(2,1)S(1)} %expert.1), channel_id=1, replica_groups=mesh['dp'=4,'expert'=8] {'dp','expert'}, dimensions={0} | all-to-all | bytes 524288 | tf_op jit(solution)/shard_map/all_to_all | solution.py:375
  65.0 1.3 %combine.1 = bf16[2,1,8,512]{3,2,1,0:T(8,128)(2,1)} custom-call(bf16[32,8,512]{2,1,0:T(8,128)(2,1)S(1)} %all_to_all.17.recv_ref, f32[32,64]{1,0:T(8,128)S(1)} %get-tuple-element.11.place_ref, f32[16,512]{1,0:T(8,128)S(1)} %get-tuple-element.14.attn_ref, bf16[2,1,8,512]{3,2,1,0:T(8,128)(2,1)S(1)} %copy-done, s32[1,2]{1,0:T(1,128)S(1)} %bitcast.17), custom_call_target="tpu_custom_call" | custom-call | flops 67108864 | bytes 1048576 | tf_op jit(solution)/shard_map/combine/pallas_call | solution.py:320
  (2 shorter events, 0.0 us)
Async XLA Ops:
  1.3 18.1 %copy-start = (bf16[2,1,8,512]{3,2,1,0:T(8,128)(2,1)S(1)}, bf16[2,1,8,512]{3,2,1,0:T(8,128)(2,1)}, u32[]{:S(2)}) copy-start(bf16[2,1,8,512]{3,2,1,0:T(8,128)(2,1)} %res_ref.3) | copy-start | bytes 49156
  1.3 18.1 %copy-start.1 = (s32[2,1]{0,1:T(1,128)S(1)}, s32[2,1]{0,1:T(1,128)}, u32[]{:S(2)}) copy-start(s32[2,1]{0,1:T(1,128)} %param.31) | copy-start | bytes 28
  1.3 18.1 %copy-start.2 = (f32[512,8]{0,1:T(8,128)S(1)}, f32[512,8]{0,1:T(8,128)}, u32[]{:S(2)}) copy-start(f32[512,8]{0,1:T(8,128)} %param.25) | copy-start | bytes 49156
  1.3 18.1 %copy-start.3 = (f32[512]{0:T(512)S(1)}, f32[512]{0:T(512)}, u32[]{:S(2)}) copy-start(f32[512]{0:T(512)} %param.24) | copy-start | bytes 6148
  1.3 34.1 %slice-start = ((s8[29360128]{0:T(1024)(128)(4,1)}), s8[4194304]{0:T(1024)(128)(4,1)S(1)}, s32[]{:S(2)}) async-start(s8[29360128]{0:T(1024)(128)(4,1)} %bitcast.10), calls=%async_computation.3 | async-start | bytes 8388608
  1.3 34.1 %slice-start.1 = ((s8[29360128]{0:T(1024)(128)(4,1)}), s8[4194304]{0:T(1024)(128)(4,1)S(1)}, s32[]{:S(2)}) async-start(s8[29360128]{0:T(1024)(128)(4,1)} %bitcast.10), calls=%async_computation.4 | async-start | bytes 8388608
  1.3 34.1 %slice-start.2 = ((s8[29360128]{0:T(1024)(128)(4,1)}), s8[4194304]{0:T(1024)(128)(4,1)S(1)}, s32[]{:S(2)}) async-start(s8[29360128]{0:T(1024)(128)(4,1)} %bitcast.10), calls=%async_computation.5 | async-start | bytes 8388608
  1.4 34.1 %slice-start.3 = ((s8[29360128]{0:T(1024)(128)(4,1)}), s8[4194304]{0:T(1024)(128)(4,1)S(1)}, s32[]{:S(2)}) async-start(s8[29360128]{0:T(1024)(128)(4,1)} %bitcast.10), calls=%async_computation.6 | async-start | bytes 8388608
  1.4 34.1 %slice-start.7 = ((s8[29360128]{0:T(1024)(128)(4,1)}), s8[4194304]{0:T(1024)(128)(4,1)S(1)}, s32[]{:S(2)}) async-start(s8[29360128]{0:T(1024)(128)(4,1)} %bitcast.13), calls=%async_computation.10 | async-start | bytes 8388608
  1.4 34.1 %slice-start.8 = ((s8[29360128]{0:T(1024)(128)(4,1)}), s8[4194304]{0:T(1024)(128)(4,1)S(1)}, s32[]{:S(2)}) async-start(s8[29360128]{0:T(1024)(128)(4,1)} %bitcast.13), calls=%async_computation.11 | async-start | bytes 8388608
  1.4 34.1 %slice-start.9 = ((s8[29360128]{0:T(1024)(128)(4,1)}), s8[4194304]{0:T(1024)(128)(4,1)S(1)}, s32[]{:S(2)}) async-start(s8[29360128]{0:T(1024)(128)(4,1)} %bitcast.13), calls=%async_computation.12 | async-start | bytes 8388608
  1.4 34.1 %slice-start.10 = ((s8[29360128]{0:T(1024)(128)(4,1)}), s8[4194304]{0:T(1024)(128)(4,1)S(1)}, s32[]{:S(2)}) async-start(s8[29360128]{0:T(1024)(128)(4,1)} %bitcast.13), calls=%async_computation.13 | async-start | bytes 8388608
  19.4 16.1 %slice-start.4 = ((s8[29360128]{0:T(1024)(128)(4,1)}), s8[4194304]{0:T(1024)(128)(4,1)S(1)}, s32[]{:S(2)}) async-start(s8[29360128]{0:T(1024)(128)(4,1)} %bitcast.10), calls=%async_computation.7 | async-start | bytes 8388608
  19.4 16.1 %slice-start.5 = ((s8[29360128]{0:T(1024)(128)(4,1)}), s8[4194304]{0:T(1024)(128)(4,1)S(1)}, s32[]{:S(2)}) async-start(s8[29360128]{0:T(1024)(128)(4,1)} %bitcast.10), calls=%async_computation.8 | async-start | bytes 8388608
  19.4 16.1 %slice-start.6 = ((s8[29360128]{0:T(1024)(128)(4,1)}), s8[4194304]{0:T(1024)(128)(4,1)S(1)}, s32[]{:S(2)}) async-start(s8[29360128]{0:T(1024)(128)(4,1)} %bitcast.10), calls=%async_computation.9 | async-start | bytes 8388608
  19.5 16.1 %slice-start.11 = ((s8[29360128]{0:T(1024)(128)(4,1)}), s8[4194304]{0:T(1024)(128)(4,1)S(1)}, s32[]{:S(2)}) async-start(s8[29360128]{0:T(1024)(128)(4,1)} %bitcast.13), calls=%async_computation.14 | async-start | bytes 8388608
  19.5 16.1 %slice-start.12 = ((s8[29360128]{0:T(1024)(128)(4,1)}), s8[4194304]{0:T(1024)(128)(4,1)S(1)}, s32[]{:S(2)}) async-start(s8[29360128]{0:T(1024)(128)(4,1)} %bitcast.13), calls=%async_computation.15 | async-start | bytes 8388608
  19.5 16.1 %slice-start.13 = ((s8[29360128]{0:T(1024)(128)(4,1)}), s8[4194304]{0:T(1024)(128)(4,1)S(1)}, s32[]{:S(2)}) async-start(s8[29360128]{0:T(1024)(128)(4,1)} %bitcast.13), calls=%async_computation.16 | async-start | bytes 8388608

commit v3 on v2

--- a/solution.py
+++ b/solution.py
@@ -42,7 +42,7 @@
     )
 
 
-def attention(queries, keys, values, new_keys, new_values, lengths, answers, routes, o_proj, peers, capacity, samples):
+def attention(queries, keys, values, new_keys, new_values, lengths, answers, routes, stops, o_proj, capacity, samples):
     _, _, steps, width = queries.shape
     table_rows = steps * samples
     slot_count = steps * capacity
@@ -61,10 +61,12 @@
         len_ref,
         ans_ref,
         routes_ref,
+        stop_ref,
         o_hbm,
         out_ref,
         place_ref,
         expert_ref,
+        active_ref,
         o_ref,
         q_s,
         a_s,
@@ -79,6 +81,8 @@
         for i in range(steps * E):
             used[i] = 0
         for t in range(steps):
+            active = jnp.full((samples, LANES), (1 - stop_ref[0, t]).astype(F32))
+            active_ref[t * samples : (t + 1) * samples, :] = active
 
             def one(s, _):
                 for k in range(TOP):
@@ -123,19 +127,18 @@
         lane = lax.broadcasted_iota(jnp.int32, (1, ANSWERS), 1)
         for t in range(steps):
             a_s[t : t + 1, width:] = (lane == ans_ref[0, 0, t]).astype(F32)
-        payload = a_s[...].astype(BF)
-        for i in range(peers):
-            out_ref[i] = payload
+        out_ref[...] = a_s[...].astype(BF)
         move.wait()
 
     return pl.pallas_call(
         body,
-        in_specs=[VM, VM, VM, VM, VM, SM, SM, SM, AN],
-        out_specs=[VM] * 4,
+        in_specs=[VM, VM, VM, VM, VM, SM, SM, SM, SM, AN],
+        out_specs=[VM] * 5,
         out_shape=[
-            jax.ShapeDtypeStruct((peers, steps, width + ANSWERS), BF),
+            pltpu.VMEM((steps, width + ANSWERS), BF),
             jax.ShapeDtypeStruct((TOP * table_rows, E * slot_count), F32),
             jax.ShapeDtypeStruct((TOP * table_rows, LANES), F32),
+            jax.ShapeDtypeStruct((table_rows, LANES), F32),
             pltpu.VMEM(o_proj.shape, o_proj.dtype),
         ],
         scratch_shapes=[
@@ -145,15 +148,31 @@
             pltpu.SemaphoreType.DMA,
         ],
         name="attention",
-        **params(1 << 36, 2),
+        **params(1 << 20, 2),
     )(
         *[parked(x) for x in (queries, keys, values, new_keys, new_values)],
         lengths,
-        *[parked(x) for x in (answers, routes, o_proj)],
-    )
-
-
-def projection(recv, o_proj, residual, gain, router, places, experts, stops, groups, spread):
+        *[parked(x) for x in (answers, routes, stops, o_proj)],
+    )
+
+
+def repeated(payload, peers):
+    def body(in_ref, out_ref):
+        row = in_ref[...]
+        for i in range(peers):
+            out_ref[i] = row
+
+    return pl.pallas_call(
+        body,
+        in_specs=[VM],
+        out_specs=VM,
+        out_shape=pltpu.VMEM((peers, *payload.shape), payload.dtype),
+        name="repeated",
+        **params(1 << 36, 2),
+    )(held(payload))
+
+
+def projection(recv, o_proj, residual, gain, router, places, experts, active, groups, spread):
     peers, steps, wide = recv.shape
     width = wide - ANSWERS
     columns = o_proj.shape[1]
@@ -164,7 +183,18 @@
     payload = columns + LANES
 
     def body(
-        recv_ref, o_ref, res_ref, gain_ref, router_ref, place_ref, expert_ref, stop_ref, out_ref, attn_ref, vote_ref
+        recv_ref,
+        o_ref,
+        res_ref,
+        gain_ref,
+        router_ref,
+        place_ref,
+        expert_ref,
+        active_ref,
+        out_ref,
+        base_ref,
+        pick_ref,
+        vote_ref,
     ):
         x = jnp.concatenate([recv_ref[i] for i in range(peers)], 0)
         to = lax.broadcasted_iota(jnp.int32, (rows, rows), 0)
@@ -174,12 +204,17 @@
         tally = jnp.zeros((1, ANSWERS), F32)
         for t in range(steps):
             hits = jnp.sum(x[t * samples : (t + 1) * samples, width:], 0, keepdims=True)
-            tally = tally + (1 - stop_ref[0, t]).astype(F32) * hits
+            tally = tally + active_ref[t * samples : t * samples + 1, :] * hits
             vote_ref[t] = tally / jnp.maximum(jnp.sum(tally, -1, keepdims=True), 1.0)
         attn = contract(x[:, :width].astype(BF), o_ref[...], 1, 0)
-        attn_ref[...] = attn
         residual = jnp.concatenate([res_ref[t, 0].astype(F32) for t in range(steps)], 0)
         mixed = residual + attn
+        active = active_ref[:, :1]
+        base_ref[...] = residual + active * attn
+        pick = place_ref[:rows, :]
+        for k in range(1, TOP):
+            pick = pick + place_ref[k * rows : (k + 1) * rows, :]
+        pick_ref[...] = active * pick
         squares = jnp.sum(mixed * mixed, -1, keepdims=True)
         scaled = mixed * gain_ref[...]
         logits = lax.dot_general(
@@ -210,16 +245,17 @@
 
     return pl.pallas_call(
         body,
-        in_specs=[VM] * 7 + [SM],
-        out_specs=[VM] * 3,
+        in_specs=[VM] * 8,
+        out_specs=[VM] * 4,
         out_shape=[
             jax.ShapeDtypeStruct((groups * peers, slot_count, payload), BF),
-            jax.ShapeDtypeStruct((rows, columns), F32),
-            jax.ShapeDtypeStruct((steps, 1, ANSWERS), F32),
+            pltpu.VMEM((rows, columns), F32),
+            pltpu.VMEM((rows, slots), F32),
+            pltpu.VMEM((steps, 1, ANSWERS), F32),
         ],
         name="projection",
         **params(1 << 36, 2 + mebi(2 * groups * peers * slot_count * payload * 2)),
-    )(recv, held(o_proj), held(residual), held(gain), held(router), places, experts, stops)
+    )(recv, held(o_proj), held(residual), held(gain), held(router), places, experts, active)
 
 
 def expert(recv, gate, up, down, peers, columns):
@@ -293,38 +329,30 @@
     )(held(recv), held(gate), held(up), parked(down))
 
 
-def combine(recv, places, attn, residual, stops, groups, spread):
-    steps, _, samples, columns = residual.shape
+def combine(recv, picks, base, votes, shape, groups, spread):
+    steps, _, samples, columns = shape
     rows = steps * samples
     peers = E * spread
 
-    def body(recv_ref, place_ref, attn_ref, res_ref, stop_ref, out_ref):
-        pick = place_ref[:rows, :]
-        for k in range(1, TOP):
-            pick = pick + place_ref[k * rows : (k + 1) * rows, :]
-        pick = pick.astype(BF)
-        moe = jnp.zeros((rows, columns), F32)
+    def body(recv_ref, pick_ref, base_ref, vote_ref, out_ref, share_ref):
+        share_ref[...] = vote_ref[...]
+        pick = pick_ref[...].astype(BF)
+        total = base_ref[...]
         for group in range(groups):
             for copy in range(spread):
                 mine = jnp.concatenate([recv_ref[group * peers + e * spread + copy] for e in range(E)], 0)
-                moe = moe + contract_rows(pick, mine)
-        update = attn_ref[...] + moe
+                total = total + contract(pick, mine, 1, 0)
         for t in range(steps):
-            active = (1 - stop_ref[0, t]).astype(F32)
-            fresh = res_ref[t, 0].astype(F32) + active * update[t * samples : (t + 1) * samples, :]
-            out_ref[t, 0] = fresh.astype(BF)
-
-    def contract_rows(pick, mine):
-        return contract(pick, mine, 1, 0)
+            out_ref[t, 0] = total[t * samples : (t + 1) * samples, :].astype(BF)
 
     return pl.pallas_call(
         body,
-        in_specs=[VM] * 4 + [SM],
-        out_specs=VM,
-        out_shape=jax.ShapeDtypeStruct(residual.shape, BF),
+        in_specs=[VM] * 4,
+        out_specs=[VM] * 2,
+        out_shape=[jax.ShapeDtypeStruct(shape, BF), jax.ShapeDtypeStruct(votes.shape, F32)],
         name="combine",
         **params(1 << 26, 3 + mebi(2 * recv.size * 2)),
-    )(recv, places, attn, held(residual), stops)
+    )(recv, held(picks), held(base), held(votes))
 
 
 def on_device(
@@ -351,8 +379,7 @@
     samples, columns = residual_in.shape[2:]
     capacity = 2 * residual_in.shape[1] * samples * TOP // E
     gate, up = expert_gate.reshape(expert_gate.shape[1:]), expert_up.reshape(expert_up.shape[1:])
-    stops = stop_mask.T
-    payload, places, experts, o_v = attention(
+    payload, places, experts, active, o_v = attention(
         jnp.transpose(queries, (1, 2, 0, 3)),
         cache_keys,
         cache_values,
@@ -361,20 +388,20 @@
         cache_len,
         jnp.transpose(answers, (1, 2, 0)),
         jnp.transpose(routes, (0, 1, 3, 2)),
+        stop_mask.T,
         o_proj,
-        peers,
         capacity,
         samples,
     )
-    recv = lax.all_to_all(payload, "expert", split_axis=0, concat_axis=0, tiled=True)
-    outgoing, attn, votes = projection(
-        recv, o_v, residual_in, norm_gain.reshape(1, columns), router.T, places, experts, stops, groups, spread
+    recv = lax.all_to_all(repeated(payload, peers), "expert", split_axis=0, concat_axis=0, tiled=True)
+    outgoing, base, picks, votes = projection(
+        recv, o_v, residual_in, norm_gain.reshape(1, columns), router.T, places, experts, active, groups, spread
     )
     tokens = lax.all_to_all(outgoing, ("dp", "expert"), split_axis=0, concat_axis=0, tiled=True)
     partial = expert(tokens, gate, up, expert_down, peers, columns)
     returned = lax.all_to_all(partial, ("dp", "expert"), split_axis=0, concat_axis=0, tiled=True)
-    updated = combine(returned, places, attn, residual_in, stops, groups, spread)
-    return updated, votes
+    updated, shares = combine(returned, picks, base, votes, residual_in.shape, groups, spread)
+    return updated, shares
 
 
 def solution(mesh):

time: 66.5 us -> 64.3 us (0.967)
  Pallas kernels: 23.8 us -> 21.5 us
    pallas_call x3 -> x4, Pallas kernels: 6.98 us -> 4.71 us  [the longest x1 2.95 us: attention(): pl.pallas_call(body, in_specs=[VM, VM, VM, VM, VM, SM, SM, SM, SM, AN], o...]
where the time goes in v3:
time: 64.3 us; the launch traced here: 64 us
  blocking collectives  40.9 us (64%)
  Pallas kernels  21.5 us (33%)
  between operations  1.56 us (2%)
    pallas_call x1, Pallas kernels, expert(): pl.pallas_call(body, in_specs=[VM, VM, VM, AN], out_specs=VM, out_shape=p...  16.8 us
    all_to_all x1, blocking collectives, on_device(): lax.all_to_all(repeated(payload, peers), 'expert', split_axis=0, concat_a...  14.3 us
    all_to_all x1, blocking collectives, on_device(): lax.all_to_all(outgoing, ('dp', 'expert'), split_axis=0, concat_axis=0, t...  14 us
    all_to_all x1, blocking collectives, on_device(): lax.all_to_all(partial, ('dp', 'expert'), split_axis=0, concat_axis=0, ti...  12.6 us
    pallas_call x1, Pallas kernels, attention(): pl.pallas_call(body, in_specs=[VM, VM, VM, VM, VM, SM, SM, SM, SM, AN], o...  2.95 us

profile of v3, /device:TPU:0, one launch (start us, length us, event | category | flops | bytes accessed | tf_op | source)
XLA Modules:
  0.0 64.0 jit_solution(14356043336069866692)
XLA Ops:
  1.3 3.0 %attention.1 = (bf16[2,2176]{1,0:T(2,128)(2,1)S(1)}, f32[32,64]{1,0:T(8,128)S(1)}, f32[32,128]{1,0:T(8,128)S(1)}, f32[16,128]{1,0:T(8,128)S(1)}, bf16[2048,512]{1,0:T(8,128)(2,1)S(1)}) custom-call(bf16[1,1,2,2048]{3,2,1,0:T(2,128)(2,1)} %bitcast.18, bf16[1,1,512,512]{3,2,1,0:T(8,128)(2,1)} %k_ref.1, bf16[1,1,512,512]{3,2,1,0:T(8,128)(2,1)} %v_ref.1, ...), custom_call_target="tpu_custom_call" | custom-call | flops 1048576 | bytes 1048576 | tf_op jit(solution)/shard_map/attention/pallas_call | solution.py:133
  4.2 0.0 copy-start
  4.2 0.0 copy-start.1
  4.3 0.0 copy-start.2
  4.3 0.0 slice-start
  4.3 0.0 slice-start.1
  4.3 0.0 slice-start.2
  4.3 0.0 slice-start.3
  4.3 0.0 slice-start.7
  4.3 0.0 slice-start.8
  4.3 0.0 slice-start.9
  4.4 0.0 slice-start.10
  4.4 14.3 %all_to_all.15.recv_ref = bf16[8,2,2176]{2,1,0:T(2,128)(2,1)S(1)} all-to-all(bf16[8,2,2176]{2,1,0:T(2,128)(2,1)S(1)} %repeated.1), channel_id=1, replica_groups=mesh['dp'=4,'expert'=8] {'expert'}, dimensions={0} | all-to-all | bytes 139264 | tf_op jit(solution)/shard_map/all_to_all | solution.py:396
  18.7 0.0 copy-done
  18.7 0.0 copy-done.1
  18.7 0.0 copy-done.2
  18.7 0.0 slice-start.4
  18.7 0.0 slice-start.5
  18.7 0.0 slice-start.6
  18.7 0.0 slice-start.11
  18.7 0.0 slice-start.12
  18.8 0.0 slice-start.13
  18.8 1.0 %projection.1 = (bf16[32,8,640]{2,1,0:T(8,128)(2,1)S(1)}, f32[16,512]{1,0:T(8,128)S(1)}, f32[16,64]{1,0:T(8,128)S(1)}, f32[2,1,128]{2,1,0:T(1,128)S(1)}) custom-call(bf16[8,2,2176]{2,1,0:T(2,128)(2,1)S(1)} %all_to_all.15.recv_ref, bf16[2048,512]{1,0:T(8,128)(2,1)S(1)} %get-tuple-element.12.o_ref, bf16[2,1,8,512]{3,2,1,0:T(8,128)(2,1)S(1)} %copy-done, ...), custom_call_target="tpu_custom_call" | custom-call | flops 68719476736 | bytes 1048576 | tf_op jit(solution)/shard_map/projection/pallas_call | solution.py:246
  19.8 14.0 %all_to_all.16.recv_ref = bf16[32,8,640]{2,1,0:T(8,128)(2,1)S(1)} all-to-all(bf16[32,8,640]{2,1,0:T(8,128)(2,1)S(1)} %get-tuple-element.16), channel_id=1, replica_groups=mesh['dp'=4,'expert'=8] {'dp','expert'}, dimensions={0} | all-to-all | bytes 655360 | tf_op jit(solution)/shard_map/all_to_all | solution.py:400
  33.8 0.0 slice-done
  33.8 0.0 slice-done.1
  33.8 0.0 slice-done.2
  33.8 0.0 slice-done.3
  33.8 0.0 slice-done.7
  33.8 0.0 slice-done.8
  33.8 0.0 slice-done.9
  33.8 0.0 slice-done.10
  33.8 0.0 slice-done.4
  33.8 0.0 slice-done.5
  33.8 0.0 slice-done.6
  33.8 0.0 slice-done.11
  33.9 0.0 slice-done.12
  33.9 0.0 slice-done.13
  33.9 16.8 %expert.1 = bf16[32,8,512]{2,1,0:T(8,128)(2,1)S(1)} custom-call(bf16[32,8,640]{2,1,0:T(8,128)(2,1)S(1)} %all_to_all.16.recv_ref, bf16[4096,3584]{1,0:T(8,128)(2,1)S(1)} %bitcast.12, bf16[4096,3584]{1,0:T(8,128)(2,1)S(1)} %bitcast.15, bf16[1,3584,4096]{2,1,0:T(8,128)(2,1)} %down_hbm.1), custom_call_target="tpu_custom_call" | custom-call | flops 8589934592 | bytes 1048576 | tf_op jit(solution)/shard_map/expert/pallas_call | solution.py:316
  50.7 12.6 %all_to_all.17.recv_ref = bf16[32,8,512]{2,1,0:T(8,128)(2,1)S(1)} all-to-all(bf16[32,8,512]{2,1,0:T(8,128)(2,1)S(1)} %expert.1), channel_id=1, replica_groups=mesh['dp'=4,'expert'=8] {'dp','expert'}, dimensions={0} | all-to-all | bytes 524288 | tf_op jit(solution)/shard_map/all_to_all | solution.py:402
  63.3 0.8 %combine.1 = (bf16[2,1,8,512]{3,2,1,0:T(8,128)(2,1)}, f32[2,1,128]{2,1,0:T(1,128)}) custom-call(bf16[32,8,512]{2,1,0:T(8,128)(2,1)S(1)} %all_to_all.17.recv_ref, f32[16,64]{1,0:T(8,128)S(1)} %get-tuple-element.17.pick_ref, f32[16,512]{1,0:T(8,128)S(1)} %get-tuple-element.18.base_ref, f32[2,1,128]{2,1,0:T(1,128)S(1)} %get-tuple-element.19.vote_ref), custom_call_target="tpu_custom_call" | custom-call | flops 67108864 | bytes 1048576 | tf_op jit(solution)/shard_map/combine/pallas_call | solution.py:348
  (3 shorter events, 0.0 us)
Async XLA Ops:
  4.2 14.4 %copy-start = (bf16[2,1,8,512]{3,2,1,0:T(8,128)(2,1)S(1)}, bf16[2,1,8,512]{3,2,1,0:T(8,128)(2,1)}, u32[]{:S(2)}) copy-start(bf16[2,1,8,512]{3,2,1,0:T(8,128)(2,1)} %res_ref.1) | copy-start | bytes 49156
  4.2 14.4 %copy-start.1 = (f32[512,8]{0,1:T(8,128)S(1)}, f32[512,8]{0,1:T(8,128)}, u32[]{:S(2)}) copy-start(f32[512,8]{0,1:T(8,128)} %param.25) | copy-start | bytes 49156
  4.3 14.4 %copy-start.2 = (f32[512]{0:T(512)S(1)}, f32[512]{0:T(512)}, u32[]{:S(2)}) copy-start(f32[512]{0:T(512)} %param.24) | copy-start | bytes 6148
  4.3 29.5 %slice-start = ((s8[29360128]{0:T(1024)(128)(4,1)}), s8[4194304]{0:T(1024)(128)(4,1)S(1)}, s32[]{:S(2)}) async-start(s8[29360128]{0:T(1024)(128)(4,1)} %bitcast.10), calls=%async_computation.3 | async-start | bytes 8388608
  4.3 29.5 %slice-start.1 = ((s8[29360128]{0:T(1024)(128)(4,1)}), s8[4194304]{0:T(1024)(128)(4,1)S(1)}, s32[]{:S(2)}) async-start(s8[29360128]{0:T(1024)(128)(4,1)} %bitcast.10), calls=%async_computation.4 | async-start | bytes 8388608
  4.3 29.5 %slice-start.2 = ((s8[29360128]{0:T(1024)(128)(4,1)}), s8[4194304]{0:T(1024)(128)(4,1)S(1)}, s32[]{:S(2)}) async-start(s8[29360128]{0:T(1024)(128)(4,1)} %bitcast.10), calls=%async_computation.5 | async-start | bytes 8388608
  4.3 29.5 %slice-start.3 = ((s8[29360128]{0:T(1024)(128)(4,1)}), s8[4194304]{0:T(1024)(128)(4,1)S(1)}, s32[]{:S(2)}) async-start(s8[29360128]{0:T(1024)(128)(4,1)} %bitcast.10), calls=%async_computation.6 | async-start | bytes 8388608
  4.3 29.5 %slice-start.7 = ((s8[29360128]{0:T(1024)(128)(4,1)}), s8[4194304]{0:T(1024)(128)(4,1)S(1)}, s32[]{:S(2)}) async-start(s8[29360128]{0:T(1024)(128)(4,1)} %bitcast.13), calls=%async_computation.10 | async-start | bytes 8388608
  4.3 29.4 %slice-start.8 = ((s8[29360128]{0:T(1024)(128)(4,1)}), s8[4194304]{0:T(1024)(128)(4,1)S(1)}, s32[]{:S(2)}) async-start(s8[29360128]{0:T(1024)(128)(4,1)} %bitcast.13), calls=%async_computation.11 | async-start | bytes 8388608
  4.3 29.4 %slice-start.9 = ((s8[29360128]{0:T(1024)(128)(4,1)}), s8[4194304]{0:T(1024)(128)(4,1)S(1)}, s32[]{:S(2)}) async-start(s8[29360128]{0:T(1024)(128)(4,1)} %bitcast.13), calls=%async_computation.12 | async-start | bytes 8388608
  4.4 29.4 %slice-start.10 = ((s8[29360128]{0:T(1024)(128)(4,1)}), s8[4194304]{0:T(1024)(128)(4,1)S(1)}, s32[]{:S(2)}) async-start(s8[29360128]{0:T(1024)(128)(4,1)} %bitcast.13), calls=%async_computation.13 | async-start | bytes 8388608
  18.7 15.1 %slice-start.4 = ((s8[29360128]{0:T(1024)(128)(4,1)}), s8[4194304]{0:T(1024)(128)(4,1)S(1)}, s32[]{:S(2)}) async-start(s8[29360128]{0:T(1024)(128)(4,1)} %bitcast.10), calls=%async_computation.7 | async-start | bytes 8388608
  18.7 15.1 %slice-start.5 = ((s8[29360128]{0:T(1024)(128)(4,1)}), s8[4194304]{0:T(1024)(128)(4,1)S(1)}, s32[]{:S(2)}) async-start(s8[29360128]{0:T(1024)(128)(4,1)} %bitcast.10), calls=%async_computation.8 | async-start | bytes 8388608
  18.7 15.1 %slice-start.6 = ((s8[29360128]{0:T(1024)(128)(4,1)}), s8[4194304]{0:T(1024)(128)(4,1)S(1)}, s32[]{:S(2)}) async-start(s8[29360128]{0:T(1024)(128)(4,1)} %bitcast.10), calls=%async_computation.9 | async-start | bytes 8388608
  18.7 15.1 %slice-start.11 = ((s8[29360128]{0:T(1024)(128)(4,1)}), s8[4194304]{0:T(1024)(128)(4,1)S(1)}, s32[]{:S(2)}) async-start(s8[29360128]{0:T(1024)(128)(4,1)} %bitcast.13), calls=%async_computation.14 | async-start | bytes 8388608
  18.7 15.1 %slice-start.12 = ((s8[29360128]{0:T(1024)(128)(4,1)}), s8[4194304]{0:T(1024)(128)(4,1)S(1)}, s32[]{:S(2)}) async-start(s8[29360128]{0:T(1024)(128)(4,1)} %bitcast.13), calls=%async_computation.15 | async-start | bytes 8388608
  18.8 15.1 %slice-start.13 = ((s8[29360128]{0:T(1024)(128)(4,1)}), s8[4194304]{0:T(1024)(128)(4,1)S(1)}, s32[]{:S(2)}) async-start(s8[29360128]{0:T(1024)(128)(4,1)} %bitcast.13), calls=%async_computation.16 | async-start | bytes 8388608
